TPU v7x, 8 devices: a whole 2x2x1 slice. The times are simulated.
8 devices in a mesh: tp: 2 (over z, y), ep: 4 (over x, core).
Axes of the slice: x: 2, y: 2, z: 1, core: 2. Of those that a mesh axis runs over, the one named last changes fastest.
Arguments:
- x_norm: bfloat16 [4096, 1024], P(('ep', 'tp'))
- route_idx: int32 [4096, 8], P(('ep', 'tp'))
- route_slot: int32 [4096, 8], P(('ep', 'tp'))
- w_router: bfloat16 [1024, 32], replicated
- b_router: float32 [32], replicated
- w_gate_up: bfloat16 [32, 1024, 1024], P('ep', None, 'tp')
- b_gate_up: float32 [32, 1024], P('ep', 'tp')
- w_down: bfloat16 [32, 512, 1024], P('ep', 'tp')
- b_down: float32 [32, 1024], P('ep')
- d_out: bfloat16 [4096, 1024], P(('ep', 'tp'))
Outputs:
- output 1: bfloat16 [4096, 1024], P(('ep', 'tp'))
- output 2: bfloat16 [4096, 1024], P(('ep', 'tp'))
- output 3: bfloat16 [32, 1024, 1024], P('ep', None, 'tp')
- output 4: float32 [32, 1024], P('ep', 'tp')
- output 5: bfloat16 [32, 512, 1024], P('ep', 'tp')
- output 6: float32 [32, 1024], P('ep')
- output 7: float32 [1024, 32], replicated
- output 8: float32 [32], replicated
All inputs are finite; a program needn't handle non-finite values.
Results may differ from a plain program's by a relative error of at most 0.0122516.
Values are sent between devices in bfloat16 or wider.
A program may use at most 1 GiB of HBM per device.

v0:
```python
import functools
import jax
import jax.numpy as jnp
from jax import lax
from jax.experimental import pallas as pl
from jax.experimental.pallas import tpu as pltpu
from jax.sharding import PartitionSpec as P

LIMIT = 7.0
ALPHA = 1.702
BF = jnp.bfloat16
F32 = jnp.float32
TILE = 256
BACK = ((1,), (1,))
LHS = ((0,), (0,))


def dot(a, b, dims=((1,), (0,))):
    return lax.dot_general(a, b, (dims, ((), ())), preferred_element_type=F32)


def split3(v):
    top = v.astype(BF)
    rest = v - top.astype(F32)
    mid = rest.astype(BF)
    return top, mid, (rest - mid.astype(F32)).astype(BF)


def chunk_kernel(first, toks, ep_ref, xa_hbm, da_hbm, xb_hbm, db_hbm, w1_in, w2_ref, b1_ref, b2_ref, *refs):
    if first:
        split_ref, *refs = refs
    ya_hbm, dxa_hbm, yb_hbm, dxb_hbm, dg_ref, gb1_ref, gb2_ref, nt_ref, *refs = refs
    if first:
        w1_ref, *refs = refs
    else:
        w1_ref = w1_in
    xs_hbm, ds_hbm, dh_hbm, wa_hbm, *refs = refs
    xin, din, ost, wst, rst, bst, xbuf, dbuf, dhst, wast, sel, zbuf, acc, off, sems, io_sems = refs
    e = pl.program_id(0)
    n_e = pl.num_programs(0)
    half, dim = w2_ref.shape[1:]
    par = lax.rem(e, 2)
    cuts = [slice(j, j + TILE) for j in range(0, dim, TILE)]
    loads = [[pltpu.make_async_copy(x_h, xin.at[i], io_sems.at[i, 0]), pltpu.make_async_copy(d_h, din.at[i], io_sems.at[i, 1])]
             for i, (x_h, d_h) in enumerate(((xa_hbm, da_hbm), (xb_hbm, db_hbm)))]
    stores = [[pltpu.make_async_copy(ost.at[i, k], o_h, io_sems.at[i, k]) for k, o_h in enumerate(pair)]
              for i, pair in enumerate(((ya_hbm, dxa_hbm), (yb_hbm, dxb_hbm)))]

    def saves(expert, t, p):
        at = pl.ds(t * TILE, TILE)
        pairs = ((xbuf, xs_hbm), (dbuf, ds_hbm), (dhst, dh_hbm), (wast, wa_hbm))
        return [pltpu.make_async_copy(src.at[p, at], dst.at[expert, t], sems.at[p, t, k])
                for k, (src, dst) in enumerate(pairs)]

    def drain(expert, p):
        for t in range(2):
            @pl.when(nt_ref[expert] > t)
            def _():
                for copy in saves(expert, t, p):
                    copy.wait()

    @pl.when(e == 0)
    def _():
        for i in range(2):
            for copy in reversed(loads[i]):
                copy.start()
            off[i] = 0

    if first:
        w1_ref[0] = dot(w1_in[0], split_ref[...]).astype(BF)

    @pl.when(e == 0)
    def _():
        base = pl.multiple_of(ep_ref[0] * 8, 8)
        b_parts = jnp.concatenate(split3(b2_ref[...]), axis=0)
        for i in range(2):
            for copy in loads[i]:
                copy.wait()

        def prepare(i, _):
            aux = din[i, toks:, :].astype(F32)
            n = aux.shape[0] // 2
            wst[i] = aux[:n, :toks] + aux[:n, toks:] + aux[n:, :toks]
            rst[i] = aux[n:, toks:]
            local_w = wst[i, pl.ds(base, 8), :]
            local_r = rst[i, pl.ds(base, 8), :]
            w_parts = jnp.concatenate(split3(jnp.where(local_r >= 0.0, local_w, 0.0)), axis=0)
            d_all = din[i, :toks, :]
            got = dot(w_parts, d_all)
            gb2_ref[...] += got[:8] + got[8:16] + got[16:]
            got = dot(b_parts, d_all, BACK)
            bst[i] = got[:8] + got[8:16] + got[16:]
            return 0

        gb2_ref[...] = jnp.zeros_like(gb2_ref)
        lax.fori_loop(0, 2, prepare, 0)

    for p in range(2):
        @pl.when((e >= 2) & (par == p))
        def _():
            drain(e - 2, p)

    row = ep_ref[0] * n_e + e
    counts = [(jnp.max(rst[i, pl.ds(row, 1), :]) + 1.0).astype(jnp.int32) for i in range(2)]
    gb1_ref[...] = jnp.zeros_like(gb1_ref)
    b_row = b2_ref[pl.ds(e, 1), :]

    seg = TILE // 2
    parts = ((0, seg), (1, seg))
    for i in range(2):
        dg_ref[0, i:i + 1, :] = jnp.where(rst[i, pl.ds(row, 1), :] >= 0.0, bst[i, pl.ds(e, 1), :], 0.0)

    def tile(t, _):
        base = (t * seg).astype(F32)
        rows = pl.ds(pl.multiple_of(t * TILE, TILE), TILE)
        hots, w_rows, at = [], [], 0
        for i, m in parts:
            pos = lax.broadcasted_iota(jnp.int32, (m, toks), 0).astype(F32)
            hot = jnp.broadcast_to(rst[i, pl.ds(row, 1), :] - base, (m, toks)) == pos
            hot_b = jnp.where(hot, 1.0, 0.0).astype(BF)
            sel[i, pl.ds(pl.multiple_of(off[i], 128), m), :] = hot_b
            w_rows.append(jnp.sum(jnp.where(hot, jnp.broadcast_to(wst[i, pl.ds(row, 1), :], (m, toks)), 0.0), axis=1, keepdims=True))
            hots.append(hot)
            dst = pl.ds(pl.multiple_of(t * TILE + at, 128), m)
            for c in cuts:
                xbuf[par, dst, c] = dot(hot_b, xin[i, :, c]).astype(BF)
            for c in cuts:
                dbuf[par, dst, c] = dot(hot_b, din[i, :toks, c]).astype(BF)
            at += m
        w_row = jnp.concatenate(w_rows, axis=0)
        x_rows = xbuf[par, rows, :]
        gate = dot(x_rows, w1_ref[0, :, :half]) + b1_ref[0, :, :half]
        up = dot(x_rows, w1_ref[0, :, half:]) + b1_ref[0, :, half:]
        d_raw = dot(dbuf[par, rows, :], w2_ref[0], BACK)
        g = jnp.minimum(gate, LIMIT)
        u1 = jnp.clip(up, -LIMIT, LIMIT) + 1.0
        sg = jax.nn.sigmoid(ALPHA * g)
        gs = g * sg
        act = (gs * u1).astype(BF)
        act_w = act.astype(F32)
        wast[par, rows, :] = (w_row * act_w).astype(BF)
        dg_row = jnp.sum(act_w * d_raw, axis=1, keepdims=True)
        d_act = w_row * d_raw
        gate_on = jnp.where(gate < LIMIT, 1.0, jnp.where(gate == LIMIT, 0.5, 0.0))
        up_abs = jnp.abs(up)
        up_on = jnp.where(up_abs < LIMIT, 1.0, jnp.where(up_abs == LIMIT, 0.5, 0.0))
        d_gate = d_act * u1 * (sg * (1.0 + ALPHA * g * (1.0 - sg))) * gate_on
        d_up = d_act * gs * up_on
        gb1_ref[0, :, :half] += jnp.sum(d_gate, axis=0, keepdims=True)
        gb1_ref[0, :, half:] += jnp.sum(d_up, axis=0, keepdims=True)
        dhst[par, rows, :half] = d_gate.astype(BF)
        dhst[par, rows, half:] = d_up.astype(BF)
        d_hid = dhst[par, rows, :]

        def put(k, c, value):
            at = 0
            for i, m in parts:
                zbuf[k, i, pl.ds(pl.multiple_of(off[i], 128), m), c] = value[at:at + m]
                at += m

        for c in cuts:
            part = (dot(act, w2_ref[0, :, c]) + b_row[:, c]).astype(BF).astype(F32)
            put(0, c, (w_row * part).astype(BF))
        for c in cuts:
            put(1, c, dot(d_hid, w1_ref[0, c, :], BACK).astype(BF))
        for copy in saves(e, t, par):
            copy.start()
        at = 0
        for (i, m), hot in zip(parts, hots):
            dg = jnp.sum(jnp.where(hot, dg_row[at:at + m], 0.0), axis=0, keepdims=True)
            dg_ref[0, i:i + 1, :] += dg
            off[i] = off[i] + m
            at += m

        return 0

    n_pass = jnp.maximum((jnp.maximum(counts[0], counts[1]) + seg - 1) // seg, 1)
    nt_ref[e] = n_pass
    lax.fori_loop(0, n_pass, tile, 0)

    @pl.when(e == n_e - 1)
    def _():
        long = 4 * TILE

        def combine(j):
            i, k = j // 2, lax.rem(j, 2)
            total = pl.multiple_of(off[i], 128)
            acc[...] = dot(sel[i, :long, :], zbuf[k, i, :long, :], LHS)

            def step(q, _):
                at = pl.ds(pl.multiple_of(q * TILE, TILE), TILE)
                acc[...] += dot(sel[i, at, :], zbuf[k, i, at, :], LHS)
                return 0

            lax.fori_loop(4, (total + TILE - 1) // TILE, step, 0)
            ost[i, k] = acc[...].astype(BF)
            return 0

        for i in range(2):
            total = pl.multiple_of(off[i], 128)
            sel[i, pl.ds(total, TILE), :] = jnp.zeros((TILE, toks), BF)
            for k in range(2):
                zbuf[k, i, pl.ds(total, TILE), :] = jnp.zeros((TILE, dim), BF)

        def go(j, _):
            combine(j)
            for q in range(4):
                @pl.when(j == q)
                def _():
                    stores[q // 2][q % 2].start()
            return 0

        lax.fori_loop(0, 4, go, 0)
        for back in (1, 0):
            p = lax.rem(e - back, 2)
            drain(e - back, p)
        for i in range(2):
            for copy in stores[i]:
                copy.wait()


def run_chunk(ep, blocks, w1, w2, b1, b2, split=None):
    first = split is not None
    n_e, dim, wide = w1.shape
    half = w2.shape[1]
    toks, tall = blocks[0].shape[0], blocks[1].shape[0]
    whole = lambda e, ep: (0, 0)
    per_e = lambda e, ep: (e, 0, 0)
    room = n_e * TILE + TILE
    hbm = pl.BlockSpec(memory_space=pl.ANY)
    in_specs = [
        hbm, hbm, hbm, hbm,
        pl.BlockSpec((1, dim, wide), per_e),
        pl.BlockSpec((1, half, dim), per_e),
        pl.BlockSpec((1, 1, wide), per_e),
        pl.BlockSpec((n_e, dim), whole),
    ]
    out_specs = [
        hbm, hbm, hbm, hbm,
        pl.BlockSpec((1, 2, toks), per_e),
        pl.BlockSpec((1, 1, wide), per_e),
        pl.BlockSpec((n_e, dim), whole),
        pl.BlockSpec(memory_space=pltpu.SMEM),
    ]
    shape = jax.ShapeDtypeStruct
    out_shape = [
        *[shape((toks, dim), BF)] * 4, shape((n_e, 2, toks), F32),
        shape((n_e, 1, wide), F32), shape((n_e, dim), F32), shape((n_e,), jnp.int32),
    ]
    if first:
        in_specs.append(pl.BlockSpec((wide, wide), whole))
        out_specs.append(pl.BlockSpec((1, dim, wide), per_e))
        out_shape.append(shape((n_e, dim, wide), BF))
    out_specs += [hbm] * 4
    out_shape += [shape((n_e, 2, TILE, w), BF) for w in (dim, dim, wide, half)]
    got = pl.pallas_call(
        functools.partial(chunk_kernel, first, toks),
        grid_spec=pltpu.PrefetchScalarGridSpec(
            num_scalar_prefetch=1,
            grid=(n_e,),
            in_specs=in_specs,
            out_specs=out_specs,
            scratch_shapes=[
                pltpu.VMEM((2, toks, dim), BF),
                pltpu.VMEM((2, tall, dim), BF),
                pltpu.VMEM((2, 2, toks, dim), BF),
                pltpu.VMEM((2, (tall - toks) // 2, toks), F32),
                pltpu.VMEM((2, (tall - toks) // 2, toks), F32),
                pltpu.VMEM((2, n_e, toks), F32),
                pltpu.VMEM((2, 2 * TILE, dim), BF),
                pltpu.VMEM((2, 2 * TILE, dim), BF),
                pltpu.VMEM((2, 2 * TILE, wide), BF),
                pltpu.VMEM((2, 2 * TILE, half), BF),
                pltpu.VMEM((2, room, toks), BF),
                pltpu.VMEM((2, 2, room, dim), BF),
                pltpu.VMEM((toks, dim), F32),
                pltpu.SMEM((2,), jnp.int32),
                pltpu.SemaphoreType.DMA((2, 2, 4)),
                pltpu.SemaphoreType.DMA((2, 2)),
            ],
        ),
        out_shape=out_shape,
        compiler_params=pltpu.CompilerParams(dimension_semantics=('arbitrary',), vmem_limit_bytes=65000 * 1024),
        cost_estimate=pl.CostEstimate(flops=28_000_000_000, bytes_accessed=40_000_000, transcendentals=0),
        name='experts',
    )(ep, *blocks, w1, w2, b1, b2, *((split,) if first else ()))
    return got[:4], got[4:8], got[-4:], (got[8] if first else w1)


def wgrad_kernel(n_c, first_e, n_prev, nt_ref, *refs):
    hbm = [refs[k * n_c:(k + 1) * n_c] for k in range(4)]
    mix_ref = refs[4 * n_c]
    gw1_ref, gw2_ref, acc1, acc2, *bufs, sems = refs[4 * n_c + 1 + n_prev:]
    e = pl.program_id(0)
    n_e = pl.num_programs(0)
    par = lax.rem(e, 2)

    def fetches(step, c, t, p):
        return [pltpu.make_async_copy(hbm[k][c].at[first_e + step, t], bufs[k].at[p, 2 * c + t], sems.at[p, 2 * c + t, k])
                for k in range(4)]

    def each(step, act):
        for c in range(n_c):
            for t in range(2):
                pl.when(nt_ref[c, first_e + step] > t)(functools.partial(act, c, t))

    def start(step, p):
        def go(c, t):
            for copy in fetches(step, c, t, p):
                copy.start()

        each(step, go)

    @pl.when(e == 0)
    def _():
        start(e, par)

    @pl.when(e + 1 < n_e)
    def _():
        start(e + 1, 1 - par)

    acc1[...] = jnp.zeros_like(acc1)
    acc2[...] = jnp.zeros_like(acc2)

    def add(j, _):
        @pl.when(nt_ref[j // 2, first_e + e] > lax.rem(j, 2))
        def _():
            for k in range(4):
                pltpu.make_async_copy(hbm[k][0].at[0, 0], bufs[k].at[par, j], sems.at[par, j, k]).wait()
            x_rows, d_rows, d_hid, act_w = (buf[par, j] for buf in bufs)
            acc1[...] += dot(x_rows, d_hid, LHS)
            acc2[...] += dot(act_w, d_rows, LHS)

        return 0

    lax.fori_loop(0, 2 * n_c, add, 0)
    gw2_ref[0] = acc2[...].astype(BF)
    gw1_ref[0] = dot(acc1[...].astype(BF), mix_ref[...]).astype(BF)


def run_wgrad(nt, saved, unmix, first_e, n_e, all_e, prev=()):
    n_c = len(saved)
    xs, ds, dh, wa = (list(t) for t in zip(*saved))
    dim, wide, half = xs[0].shape[3], dh[0].shape[3], wa[0].shape[3]
    return pl.pallas_call(
        functools.partial(wgrad_kernel, n_c, first_e, len(prev)),
        grid_spec=pltpu.PrefetchScalarGridSpec(
            num_scalar_prefetch=1,
            grid=(n_e,),
            in_specs=[pl.BlockSpec(memory_space=pl.ANY)] * (4 * n_c) + [pl.BlockSpec((wide, wide), lambda e, nt: (0, 0))]
            + [pl.BlockSpec(memory_space=pl.ANY)] * len(prev),
            out_specs=[pl.BlockSpec((1, dim, wide), lambda e, nt: (first_e + e, 0, 0)), pl.BlockSpec((1, half, dim), lambda e, nt: (first_e + e, 0, 0))],
            scratch_shapes=[pltpu.VMEM((dim, wide), F32), pltpu.VMEM((half, dim), F32)]
            + [pltpu.VMEM((2, 2 * n_c, TILE, w), BF) for w in (dim, dim, wide, half)]
            + [pltpu.SemaphoreType.DMA((2, 2 * n_c, 4))],
        ),
        out_shape=[jax.ShapeDtypeStruct((all_e, dim, wide), BF), jax.ShapeDtypeStruct((all_e, half, dim), BF)],
        input_output_aliases={4 * n_c + 2 + k: k for k in range(len(prev))},
        compiler_params=pltpu.CompilerParams(dimension_semantics=('arbitrary',), vmem_limit_bytes=64000 * 1024),
        cost_estimate=pl.CostEstimate(flops=26_000_000_000, bytes_accessed=60_000_000, transcendentals=0),
        name='weight_grads',
    )(nt, *xs, *ds, *dh, *wa, unmix, *prev)


def pack_kernel(x_ref, d_ref, idx_ref, slot_ref, wr_ref, br_ref, tall_ref, w_ref):
    toks = x_ref.shape[0]
    top_k, n = idx_ref.shape[0], wr_ref.shape[0]
    logits = dot(wr_ref[...], x_ref[...], BACK) + br_ref[...]
    expert = lax.broadcasted_iota(jnp.int32, (n, toks), 0)
    hots = [jnp.broadcast_to(idx_ref[k:k + 1, :], (n, toks)) == expert for k in range(top_k)]
    picked = [jnp.sum(jnp.where(h, logits, 0.0), axis=0, keepdims=True) for h in hots]
    top = functools.reduce(jnp.maximum, picked)
    exps = [jnp.exp(v - top) for v in picked]
    norm = functools.reduce(jnp.add, exps)
    w_full = jnp.zeros((n, toks), F32)
    kept = jnp.zeros((n, toks), F32)
    for k in range(top_k):
        w_full += jnp.where(hots[k], exps[k] / norm, 0.0)
        kept += jnp.where(hots[k], jnp.where(slot_ref[k:k + 1, :] >= 0, 1.0, 0.0), 0.0)
    w_ref[...] = w_full
    ahead = lax.broadcasted_iota(jnp.int32, (toks, toks), 0) < lax.broadcasted_iota(jnp.int32, (toks, toks), 1)
    rank = dot(kept.astype(BF), jnp.where(ahead, 1.0, 0.0).astype(BF))
    rank = jnp.where(kept > 0.0, rank, -1.0)
    w_top = w_full.astype(BF)
    rest = w_full - w_top.astype(F32)
    w_mid = rest.astype(BF)
    w_low = (rest - w_mid.astype(F32)).astype(BF)
    tall_ref[:toks, :] = d_ref[...]
    tall_ref[toks:toks + n, :toks] = w_top
    tall_ref[toks:toks + n, toks:] = w_mid
    tall_ref[toks + n:, :toks] = w_low
    tall_ref[toks + n:, toks:] = rank.astype(BF)


def run_pack(x_loc, dy_loc, idx_t, slot_t, w_router, b_router):
    toks, dim = x_loc.shape
    n = w_router.shape[0]
    return pl.pallas_call(
        pack_kernel,
        out_shape=[jax.ShapeDtypeStruct((toks + 2 * n, dim), BF), jax.ShapeDtypeStruct((n, toks), F32)],
        compiler_params=pltpu.CompilerParams(vmem_limit_bytes=32000 * 1024),
        name='pack',
    )(x_loc, dy_loc, idx_t, slot_t, w_router, b_router)


def router_kernel(rel, me_ref, *refs):
    n = len(rel)
    d_ref, out_ref = refs[n:]
    total = jnp.zeros(out_ref.shape, F32)
    for k in range(n):
        d_one = d_ref[me_ref[0] ^ rel[k]].astype(BF)
        total += lax.dot_general(refs[k][...], d_one, (((0,), (1,)), ((), ())), preferred_element_type=F32)
    out_ref[...] = total


def run_router_grad(me, rel, x_blocks, d_rel):
    n = len(x_blocks)
    toks, dim = x_blocks[0].shape
    experts = d_rel.shape[1]
    cut = dim // 4
    return pl.pallas_call(
        functools.partial(router_kernel, rel),
        grid_spec=pltpu.PrefetchScalarGridSpec(
            num_scalar_prefetch=1,
            grid=(4,),
            in_specs=[pl.BlockSpec((toks, cut), lambda j, me: (0, j))] * n + [pl.BlockSpec(d_rel.shape, lambda j, me: (0, 0, 0))],
            out_specs=pl.BlockSpec((cut, experts), lambda j, me: (j, 0)),
        ),
        out_shape=jax.ShapeDtypeStruct((dim, experts), F32),
        compiler_params=pltpu.CompilerParams(vmem_limit_bytes=32000 * 1024),
        name='router_grad',
    )(me, *x_blocks, d_rel)


def solution(mesh):
    tp_count = mesh.shape['tp']
    ep_count = mesh.shape['ep']
    n_dev = tp_count * ep_count
    tok_spec = P(('ep', 'tp'), None)

    CORE, XF, YF = 2, 4, 1
    FAR = XF | YF
    CHIPS = (0, YF, FAR, XF)

    def flip(arr, bits):
        turned = (bits & 1) * ep_count + (bits >> 1)
        return lax.ppermute(arr, ('tp', 'ep'), [(s, s ^ turned) for s in range(n_dev)])

    def device_fn(x_loc, idx_loc, slot_loc, w_router, b_router, w_gate_up, b_gate_up, w_down, b_down, dy_loc):
        toks, _ = x_loc.shape
        n_experts = w_router.shape[1]
        n_e = w_gate_up.shape[0]
        wide = w_gate_up.shape[2]
        half = wide // 2
        tp_index = lax.axis_index('tp')
        ep_index = lax.axis_index('ep')
        me = ep_index * tp_count + tp_index

        tall, w_full = run_pack(x_loc, dy_loc, idx_loc.T, slot_loc.T, w_router.T, b_router[:, None])

        x_of = {XF: flip(x_loc, XF), YF: flip(x_loc, YF)}
        d_of = {XF: flip(tall, XF | CORE), YF: flip(tall, YF | CORE)}
        x_of[FAR] = flip(x_of[XF], YF)
        d_of[FAR] = flip(d_of[YF], XF)
        pairs = [(x_loc, tall, flip(x_loc, CORE), flip(tall, CORE))]
        for bits in CHIPS[1:]:
            pairs.append((x_of[bits], flip(d_of[bits], CORE), flip(x_of[bits], CORE), d_of[bits]))

        col = jnp.arange(wide)
        split_mat = (jnp.where(col < half, 2 * col, 2 * (col - half) + 1)[None, :] == col[:, None]).astype(BF)
        b1 = jnp.concatenate([b_gate_up[:, 0::2], b_gate_up[:, 1::2]], axis=1)[:, None, :]
        b2 = b_down * (tp_index == 0).astype(F32)
        ep = ep_index.astype(jnp.int32)[None]

        w1 = w_gate_up
        dgs, gb1s, gb2s, nts, saved, part = [], [], [], [], [], []

        def chunk(step, blocks, w1):
            o, small, keep, w1 = run_chunk(ep, blocks, w1, w_down, b1, b2, split_mat if step == 0 else None)
            for lst, v in zip((dgs, gb1s, gb2s, nts), small):
                lst.append(v)
            saved.append(keep)
            ya, dxa, yb, dxb = o
            if step == 0:
                part.append((ya, flip(yb, CORE), dxa, flip(dxb, CORE)))
            else:
                part.append((ya, flip(yb, CORE), dxb, flip(dxa, CORE)))
            return w1

        def both(step):
            ya, yb, dxa, dxb = part[step]
            add = lambda a, b: (a.astype(F32) + b.astype(F32)).astype(BF)
            return add(ya, yb), add(dxa, dxb)

        def hop(step, y, dx):
            bits = CHIPS[step]
            return flip(y, bits), flip(dx, bits | CORE)

        w1 = chunk(0, pairs[0], w_gate_up)
        w1 = chunk(1, pairs[1], w1)
        sum_1, blocks = lax.optimization_barrier((both(1), pairs[2]))
        got_1 = hop(1, *sum_1)
        w1 = chunk(2, blocks, w1)
        sum_2, blocks = lax.optimization_barrier((both(2), pairs[3]))
        got_2 = hop(2, *sum_2)
        chunk(3, blocks, w1)

        rel = [CHIPS[k // 2] ^ (CORE * (k % 2)) for k in range(n_dev)]
        dg_rel = jnp.stack([dg[:, k, :] for dg in dgs for k in range(2)])
        slot_of = jnp.array([rel.index(m) for m in range(n_dev)], jnp.int32)
        dg_abs = dg_rel[slot_of[jnp.arange(n_dev) ^ me]]
        dg_back = lax.all_to_all(dg_abs, ('ep', 'tp'), 0, 0, tiled=True)
        nt_all = jnp.stack(nts)
        unmix = split_mat.T
        part_e = n_e // 4
        grads = run_wgrad(nt_all, saved, unmix, 0, part_e, n_e)
        last, dg_back, nt_b, grads = lax.optimization_barrier((part[3], dg_back, nt_all, grads))
        part[3] = last
        d_gate = jnp.sum(dg_back.reshape(ep_count, tp_count, n_e, toks), axis=1).reshape(n_experts, toks)
        d_logits = w_full * (d_gate - jnp.sum(w_full * d_gate, axis=0, keepdims=True))
        sum_3, d_logits, nt_b, grads = lax.optimization_barrier((both(3), d_logits, nt_b, grads))
        d_all = lax.all_to_all(jnp.broadcast_to(d_logits[None], (n_dev, *d_logits.shape)), ('ep', 'tp'), 0, 0, tiled=True)
        got_3 = hop(3, *sum_3)
        gw1, gw2 = run_wgrad(nt_b, saved, unmix, part_e, n_e - part_e, n_e, grads)
        gb1 = functools.reduce(jnp.add, gb1s)[:, 0, :]
        gb1 = jnp.stack([gb1[:, :half], gb1[:, half:]], axis=2).reshape(n_e, wide)
        gb2 = functools.reduce(jnp.add, gb2s)

        wide_sum = lambda *terms: functools.reduce(jnp.add, [t.astype(F32) for t in terms])
        via_router = jnp.einsum('et,de->td', d_logits.astype(BF), w_router, preferred_element_type=F32)
        d_all, gw1, own = lax.optimization_barrier((d_all, gw1, part[0]))
        gwr = run_router_grad(me.astype(jnp.int32)[None], rel, [p[k] for p in pairs for k in (0, 2)], d_all)
        gwr, got_3 = lax.optimization_barrier((gwr, got_3))
        moe = wide_sum(own[0], own[1], got_1[0], got_2[0], got_3[0])
        d_x = wide_sum(own[2], own[3], got_1[1], got_2[1], got_3[1], via_router)
        gbr = jnp.sum(d_all, axis=(0, 2))
        return (moe.astype(BF), d_x.astype(BF), gw1, gb1, gw2, gb2, gwr, gbr)

    in_specs = (tok_spec, tok_spec, tok_spec, P(None, None), P(None), P('ep', None, 'tp'), P('ep', 'tp'), P('ep', 'tp', None), P('ep', None), tok_spec)
    out_specs = (tok_spec, tok_spec, P('ep', None, 'tp'), P('ep', 'tp'), P('ep', 'tp', None), P('ep', None), P(None, None), P(None))

    return jax.shard_map(device_fn, mesh=mesh, in_specs=in_specs, out_specs=out_specs, check_vma=False)
```

profile of v0, /device:TPU:0, one launch (start us, length us, event | category | flops | bytes accessed | tf_op | source)
XLA Modules:
  0.0 366.8 jit_solution(16092031958771524081)
XLA Ops:
  4.9 1.9 pack.1
  6.8 2.8 collective-permute-start.1
  15.7 43.0 %collective-permute-done.xa_hbm.refs_2_ = bf16[512,1024]{1,0:T(8,128)(2,1)} collective-permute-done((bf16[512,1024]{1,0:T(8,128)(2,1)}, bf16[512,1024]{1,0:T(8,128)(2,1)}, u32[]{:S(2)}, u32[]{:S(2)}) %collective-permute-start) | collective-permute-done | bytes 1048608 | tf_op jit(solution)/shard_map/ppermute | solution.py:447
  58.7 2.4 collective-permute-start.9
  62.6 39.9 %experts.4 = (bf16[512,1024]{1,0:T(8,128)(2,1)}, bf16[512,1024]{1,0:T(8,128)(2,1)}, bf16[512,1024]{1,0:T(8,128)(2,1)}, bf16[512,1024]{1,0:T(8,128)(2,1)}, f32[8,...) custom-call(s32[1]{0:T(128)} %bitcast.ep_ref, ...), custom_call_target="tpu_custom_call" | custom-call | flops 28000000000 | bytes 40000000 | tf_op jit(solution)/shard_map/experts/pallas_call | solution.py:256
  102.5 34.2 %experts.5 = (bf16[512,1024]{1,0:T(8,128)(2,1)}, bf16[512,1024]{1,0:T(8,128)(2,1)}, bf16[512,1024]{1,0:T(8,128)(2,1)}, bf16[512,1024]{1,0:T(8,128)(2,1)}, f32[8,...) custom-call(s32[1]{0:T(128)} %bitcast.ep_ref, ...), custom_call_target="tpu_custom_call" | custom-call | flops 28000000000 | bytes 40000000 | tf_op jit(solution)/shard_map/experts/pallas_call | solution.py:256
  139.9 2.9 add_convert_fusion.7
  144.6 36.4 %experts.6 = (bf16[512,1024]{1,0:T(8,128)(2,1)}, bf16[512,1024]{1,0:T(8,128)(2,1)}, bf16[512,1024]{1,0:T(8,128)(2,1)}, bf16[512,1024]{1,0:T(8,128)(2,1)}, f32[8,...) custom-call(s32[1]{0:T(128)} %bitcast.ep_ref, ...), custom_call_target="tpu_custom_call" | custom-call | flops 28000000000 | bytes 40000000 | tf_op jit(solution)/shard_map/experts/pallas_call | solution.py:256
  184.2 2.6 add_convert_fusion.5
  188.3 1.9 collective-permute-done.16.da_hbm
  190.2 36.2 %experts.7 = (bf16[512,1024]{1,0:T(8,128)(2,1)}, bf16[512,1024]{1,0:T(8,128)(2,1)}, bf16[512,1024]{1,0:T(8,128)(2,1)}, bf16[512,1024]{1,0:T(8,128)(2,1)}, f32[8,...) custom-call(s32[1]{0:T(128)} %bitcast.ep_ref, ...), custom_call_target="tpu_custom_call" | custom-call | flops 28000000000 | bytes 40000000 | tf_op jit(solution)/shard_map/experts/pallas_call | solution.py:256
  228.8 2.3 all-to-all-start
  232.9 11.7 %weight_grads.2 = (bf16[8,1024,512]{2,1,0:T(8,128)(2,1)}, bf16[8,256,1024]{2,1,0:T(8,128)(2,1)}) custom-call(s32[4,8]{1,0:T(4,128)} %pad_add_fusion.nt_ref, bf16[8,2,256,1024]{3,2,1,0:T(8,128)(2,1)} %get-tuple-element.128.refs_0_, bf16[8,2,256,1024]{3,2,1,0:T(8,128)(2,1)} %get-tuple-element.129.refs_1_, ...), custom_call_target="tpu_custom_call" | custom-call | flops 25999998976 | bytes 60000000 | tf_op jit(solution)/shard_map/weight_grads/pallas_call | solution.py:345
  244.8 4.2 %add_convert_fusion.2 = (bf16[512,1024]{1,0:T(8,128)(2,1)}, bf16[512,1024]{1,0:T(8,128)(2,1)S(1)}) fusion(bf16[512,1024]{1,0:T(8,128)(2,1)} %collective-permute-done.19, bf16[512,1024]{1,0:T(8,128)(2,1)} %get-tuple-element.148, bf16[512,1024]{1,0:T(8,128)(2,1)} %collective-permute-done.18, bf16[512,1024]{1,0:T(8,128)(2,1)} %get-tuple-element.146), kind=kLoop, calls=%fused_computation.4 | loop fusion | flops 4194304 | bytes 6291456 | tf_op jit(solution)/shard_map/convert_element_type | solution.py:492
  249.0 4.7 %collective-permute-start.24 = (bf16[512,1024]{1,0:T(8,128)(2,1)S(1)}, bf16[512,1024]{1,0:T(8,128)(2,1)}, u32[]{:S(2)}, u32[]{:S(2)}) collective-permute-start(bf16[512,1024]{1,0:T(8,128)(2,1)S(1)} %get-tuple-element.169), channel_id=1, source_target_pairs={{0,2},{1,3},{2,0},{3,1},{4,6},{5,7},{6,4},{7,5}} | collective-permute-start | bytes 3145736 | tf_op jit(solution)/shard_map/ppermute | solution.py:447
  257.7 2.2 all-to-all-start.1
  259.9 2.9 collective-permute-start.23
  262.8 15.0 %collective-permute-done.24 = bf16[512,1024]{1,0:T(8,128)(2,1)} collective-permute-done((bf16[512,1024]{1,0:T(8,128)(2,1)S(1)}, bf16[512,1024]{1,0:T(8,128)(2,1)}, u32[]{:S(2)}, u32[]{:S(2)}) %collective-permute-start.24) | collective-permute-done | bytes 1048608 | tf_op jit(solution)/shard_map/ppermute | solution.py:447
  277.8 29.9 %weight_grads.3 = (bf16[8,1024,512]{2,1,0:T(8,128)(2,1)}, bf16[8,256,1024]{2,1,0:T(8,128)(2,1)}) custom-call(s32[4,8]{1,0:T(4,128)} %pad_add_fusion.nt_ref, bf16[8,2,256,1024]{3,2,1,0:T(8,128)(2,1)} %get-tuple-element.128.refs_0_, bf16[8,2,256,1024]{3,2,1,0:T(8,128)(2,1)} %get-tuple-element.129.refs_1_, ...), custom_call_target="tpu_custom_call", output_to_operand_aliasing={{0}: (18, {}), {1}: (19, {})} | custom-call | flops 25999998976 | bytes 60000000 | tf_op jit(solution)/shard_map/weight_grads/pallas_call | solution.py:345
  307.7 1.8 fusion.4
  309.5 41.0 %all-to-all-done.1.refs_8_ = f32[8,32,512]{2,1,0:T(8,128)S(1)} async-done(((f32[8,32,512]{2,1,0:T(8,128)}), f32[8,32,512]{2,1,0:T(8,128)S(1)}, u32[]{:S(2)}, u32[]{:S(2)}) %all-to-all-start.1) | async-done | bytes 524320 | tf_op jit(solution)/shard_map/all_to_all | solution.py:522
  351.2 5.6 %router_grad.1 = f32[1024,32]{1,0:T(8,128)S(1)} custom-call(s32[1]{0:T(128)} %bitcast.22.me_ref, bf16[512,1024]{1,0:T(8,128)(2,1)} %refs_0_.1, bf16[512,1024]{1,0:T(8,128)(2,1)} %collective-permute-done.4.xb_hbm.refs_1_, bf16[512,1024]{1,0:T(8,128)(2,1)} %collective-permute-done.xa_hbm.refs_2_, bf16[512,1024]{1,0:T(8,128)(2,1)} %collective-permute-done.3.xb_hbm.refs_3_, ...), custom_call_target="tpu_custom_call" | custom-call | tf_op jit(solution)/shard_map/router_grad/pallas_call | solution.py:421
  357.6 4.8 %add_convert_fusion.1 = bf16[512,1024]{1,0:T(8,128)(2,1)} fusion(bf16[512,1024]{1,0:T(8,128)(2,1)} %collective-permute-done.24, bf16[512,1024]{1,0:T(8,128)(2,1)} %collective-permute-done.23, bf16[512,1024]{1,0:T(8,128)(2,1)} %collective-permute-done.22, bf16[512,1024]{1,0:T(8,128)(2,1)} %collective-permute-done.20, bf16[512,1024]{1,0:T(8,128)(2,1)} %get-tuple-element.164), kind=kLoop, calls=%fused_computation.3 | loop fusion | flops 5242880 | bytes 6291456 | tf_op jit(solution)/shard_map/convert_element_type | solution.py:537
  362.4 4.4 %add_convert_fusion = bf16[512,1024]{1,0:T(8,128)(2,1)} fusion(f32[512,1024]{1,0:T(8,128)S(1)} %copy-done.7, bf16[512,1024]{1,0:T(8,128)(2,1)} %collective-permute-done.25, bf16[512,1024]{1,0:T(8,128)(2,1)} %collective-permute-done.27, bf16[512,1024]{1,0:T(8,128)(2,1)} %collective-permute-done.26, bf16[512,1024]{1,0:T(8,128)(2,1)} %collective-permute-done.21, ...), kind=kLoop, calls=%fused_computation.2 | loop fusion | flops 5767168 | bytes 8388608 | tf_op jit(solution)/shard_map/convert_element_type | solution.py:537
  (138 shorter events, 31.0 us)
Async XLA Ops:
  6.8 54.3 %collective-permute-start.1 = (bf16[576,1024]{1,0:T(8,128)(2,1)S(1)}, bf16[576,1024]{1,0:T(8,128)(2,1)}, u32[]{:S(2)}, u32[]{:S(2)}) collective-permute-start(bf16[576,1024]{1,0:T(8,128)(2,1)S(1)} %get-tuple-element.98.da_hbm), channel_id=1, source_target_pairs={{0,5},{1,4},{2,7},{3,6},{4,1},{5,0},{6,3},{7,2}} | collective-permute-start | bytes 3538952 | tf_op jit(solution)/shard_map/ppermute | solution.py:447
  9.6 53.0 %collective-permute-start.5 = (bf16[576,1024]{1,0:T(8,128)(2,1)S(1)}, bf16[576,1024]{1,0:T(8,128)(2,1)}, u32[]{:S(2)}, u32[]{:S(2)}) collective-permute-start(bf16[576,1024]{1,0:T(8,128)(2,1)S(1)} %get-tuple-element.98.da_hbm), channel_id=1, source_target_pairs={{0,1},{1,0},{2,3},{3,2},{4,5},{5,4},{6,7},{7,6}} | collective-permute-start | bytes 3538952 | tf_op jit(solution)/shard_map/ppermute | solution.py:447
  10.3 48.4 %collective-permute-start = (bf16[512,1024]{1,0:T(8,128)(2,1)}, bf16[512,1024]{1,0:T(8,128)(2,1)}, u32[]{:S(2)}, u32[]{:S(2)}) collective-permute-start(bf16[512,1024]{1,0:T(8,128)(2,1)} %refs_0_.1), channel_id=1, source_target_pairs={{0,4},{1,5},{2,6},{3,7},{4,0},{5,1},{6,2},{7,3}} | collective-permute-start | bytes 3145736 | tf_op jit(solution)/shard_map/ppermute | solution.py:447
  11.2 47.6 %collective-permute-start.8 = (bf16[512,1024]{1,0:T(8,128)(2,1)}, bf16[512,1024]{1,0:T(8,128)(2,1)}, u32[]{:S(2)}, u32[]{:S(2)}) collective-permute-start(bf16[512,1024]{1,0:T(8,128)(2,1)} %refs_0_.1), channel_id=1, source_target_pairs={{0,2},{1,3},{2,0},{3,1},{4,6},{5,7},{6,4},{7,5}} | collective-permute-start | bytes 3145736 | tf_op jit(solution)/shard_map/ppermute | solution.py:447
  12.6 50.0 %collective-permute-start.4 = (bf16[512,1024]{1,0:T(8,128)(2,1)}, bf16[512,1024]{1,0:T(8,128)(2,1)}, u32[]{:S(2)}, u32[]{:S(2)}) collective-permute-start(bf16[512,1024]{1,0:T(8,128)(2,1)} %refs_0_.1), channel_id=1, source_target_pairs={{0,1},{1,0},{2,3},{3,2},{4,5},{5,4},{6,7},{7,6}} | collective-permute-start | bytes 3145736 | tf_op jit(solution)/shard_map/ppermute | solution.py:447
  58.7 43.8 %collective-permute-start.3 = (bf16[512,1024]{1,0:T(8,128)(2,1)}, bf16[512,1024]{1,0:T(8,128)(2,1)}, u32[]{:S(2)}, u32[]{:S(2)}) collective-permute-start(bf16[512,1024]{1,0:T(8,128)(2,1)} %collective-permute-done.xa_hbm.refs_2_), channel_id=1, source_target_pairs={{0,1},{1,0},{2,3},{3,2},{4,5},{5,4},{6,7},{7,6}} | collective-permute-start | bytes 3145736 | tf_op jit(solution)/shard_map/ppermute | solution.py:447
  58.7 79.0 %collective-permute-start.9 = (bf16[512,1024]{1,0:T(8,128)(2,1)}, bf16[512,1024]{1,0:T(8,128)(2,1)}, u32[]{:S(2)}, u32[]{:S(2)}) collective-permute-start(bf16[512,1024]{1,0:T(8,128)(2,1)} %collective-permute-done.8.xa_hbm.refs_6_), channel_id=1, source_target_pairs={{0,4},{1,5},{2,6},{3,7},{4,0},{5,1},{6,2},{7,3}} | collective-permute-start | bytes 3145736 | tf_op jit(solution)/shard_map/ppermute | solution.py:447
  61.1 76.2 %collective-permute-start.10 = (bf16[576,1024]{1,0:T(8,128)(2,1)}, bf16[576,1024]{1,0:T(8,128)(2,1)}, u32[]{:S(2)}, u32[]{:S(2)}) collective-permute-start(bf16[576,1024]{1,0:T(8,128)(2,1)} %collective-permute-done.1.db_hbm), channel_id=1, source_target_pairs={{0,2},{1,3},{2,0},{3,1},{4,6},{5,7},{6,4},{7,5}} | collective-permute-start | bytes 3538952 | tf_op jit(solution)/shard_map/ppermute | solution.py:447
  62.6 39.9 %collective-permute-start.2 = (bf16[576,1024]{1,0:T(8,128)(2,1)}, bf16[576,1024]{1,0:T(8,128)(2,1)}, u32[]{:S(2)}, u32[]{:S(2)}) collective-permute-start(bf16[576,1024]{1,0:T(8,128)(2,1)} %collective-permute-done.1.db_hbm), channel_id=1, source_target_pairs={{0,1},{1,0},{2,3},{3,2},{4,5},{5,4},{6,7},{7,6}} | collective-permute-start | bytes 3538952 | tf_op jit(solution)/shard_map/ppermute | solution.py:447
  137.3 7.3 %collective-permute-start.11 = (bf16[576,1024]{1,0:T(8,128)(2,1)}, bf16[576,1024]{1,0:T(8,128)(2,1)}, u32[]{:S(2)}, u32[]{:S(2)}) collective-permute-start(bf16[576,1024]{1,0:T(8,128)(2,1)} %collective-permute-done.10.db_hbm), channel_id=1, source_target_pairs={{0,1},{1,0},{2,3},{3,2},{4,5},{5,4},{6,7},{7,6}} | collective-permute-start | bytes 3538952 | tf_op jit(solution)/shard_map/ppermute | solution.py:447
  137.8 44.9 %collective-permute-start.15 = (bf16[576,1024]{1,0:T(8,128)(2,1)}, bf16[576,1024]{1,0:T(8,128)(2,1)}, u32[]{:S(2)}, u32[]{:S(2)}) collective-permute-start(bf16[576,1024]{1,0:T(8,128)(2,1)} %copy-done.5), channel_id=1, source_target_pairs={{0,3},{1,2},{2,1},{3,0},{4,7},{5,6},{6,5},{7,4}} | collective-permute-start | bytes 3538952 | tf_op jit(solution)/shard_map/ppermute | solution.py:447
  182.2 77.7 %collective-permute-start.20 = (bf16[512,1024]{1,0:T(8,128)(2,1)}, bf16[512,1024]{1,0:T(8,128)(2,1)}, u32[]{:S(2)}, u32[]{:S(2)}) collective-permute-start(bf16[512,1024]{1,0:T(8,128)(2,1)} %get-tuple-element.161), channel_id=1, source_target_pairs={{0,1},{1,0},{2,3},{3,2},{4,5},{5,4},{6,7},{7,6}} | collective-permute-start | bytes 3145736 | tf_op jit(solution)/shard_map/ppermute | solution.py:447
  182.7 7.5 %collective-permute-start.16 = (bf16[576,1024]{1,0:T(8,128)(2,1)}, bf16[576,1024]{1,0:T(8,128)(2,1)}, u32[]{:S(2)}, u32[]{:S(2)}) collective-permute-start(bf16[576,1024]{1,0:T(8,128)(2,1)} %collective-permute-done.15.db_hbm), channel_id=1, source_target_pairs={{0,1},{1,0},{2,3},{3,2},{4,5},{5,4},{6,7},{7,6}} | collective-permute-start | bytes 3538952 | tf_op jit(solution)/shard_map/ppermute | solution.py:447
  183.9 78.9 %collective-permute-start.21 = (bf16[512,1024]{1,0:T(8,128)(2,1)}, bf16[512,1024]{1,0:T(8,128)(2,1)}, u32[]{:S(2)}, u32[]{:S(2)}) collective-permute-start(bf16[512,1024]{1,0:T(8,128)(2,1)} %get-tuple-element.163), channel_id=1, source_target_pairs={{0,1},{1,0},{2,3},{3,2},{4,5},{5,4},{6,7},{7,6}} | collective-permute-start | bytes 3145736 | tf_op jit(solution)/shard_map/ppermute | solution.py:447
  228.8 15.8 %all-to-all-start = ((f32[8,8,512]{2,1,0:T(8,128)}), f32[8,8,512]{2,1,0:T(8,128)S(1)}, u32[]{:S(2)}, u32[]{:S(2)}) async-start(f32[8,8,512]{2,1,0:T(8,128)} %gather_fusion.1), calls=%async_computation | async-start | bytes 262144 | tf_op jit(solution)/shard_map/all_to_all | solution.py:512
  231.1 13.5 %collective-permute-start.18 = (bf16[512,1024]{1,0:T(8,128)(2,1)}, bf16[512,1024]{1,0:T(8,128)(2,1)}, u32[]{:S(2)}, u32[]{:S(2)}) collective-permute-start(bf16[512,1024]{1,0:T(8,128)(2,1)} %get-tuple-element.117), channel_id=1, source_target_pairs={{0,1},{1,0},{2,3},{3,2},{4,5},{5,4},{6,7},{7,6}} | collective-permute-start | bytes 3145736 | tf_op jit(solution)/shard_map/ppermute | solution.py:447
  231.3 13.3 %collective-permute-start.19 = (bf16[512,1024]{1,0:T(8,128)(2,1)}, bf16[512,1024]{1,0:T(8,128)(2,1)}, u32[]{:S(2)}, u32[]{:S(2)}) collective-permute-start(bf16[512,1024]{1,0:T(8,128)(2,1)} %get-tuple-element.119), channel_id=1, source_target_pairs={{0,1},{1,0},{2,3},{3,2},{4,5},{5,4},{6,7},{7,6}} | collective-permute-start | bytes 3145736 | tf_op jit(solution)/shard_map/ppermute | solution.py:447
  249.0 28.8 %collective-permute-start.24 = (bf16[512,1024]{1,0:T(8,128)(2,1)S(1)}, bf16[512,1024]{1,0:T(8,128)(2,1)}, u32[]{:S(2)}, u32[]{:S(2)}) collective-permute-start(bf16[512,1024]{1,0:T(8,128)(2,1)S(1)} %get-tuple-element.169), channel_id=1, source_target_pairs={{0,2},{1,3},{2,0},{3,1},{4,6},{5,7},{6,4},{7,5}} | collective-permute-start | bytes 3145736 | tf_op jit(solution)/shard_map/ppermute | solution.py:447
  253.7 103.9 %collective-permute-start.22 = (bf16[512,1024]{1,0:T(8,128)(2,1)}, bf16[512,1024]{1,0:T(8,128)(2,1)}, u32[]{:S(2)}, u32[]{:S(2)}) collective-permute-start(bf16[512,1024]{1,0:T(8,128)(2,1)} %add_convert_fusion.7), channel_id=1, source_target_pairs={{0,4},{1,5},{2,6},{3,7},{4,0},{5,1},{6,2},{7,3}} | collective-permute-start | bytes 3145736 | tf_op jit(solution)/shard_map/ppermute | solution.py:447
  255.2 107.2 %collective-permute-start.26 = (bf16[512,1024]{1,0:T(8,128)(2,1)}, bf16[512,1024]{1,0:T(8,128)(2,1)}, u32[]{:S(2)}, u32[]{:S(2)}) collective-permute-start(bf16[512,1024]{1,0:T(8,128)(2,1)} %add_convert_fusion.6), channel_id=1, source_target_pairs={{0,5},{1,4},{2,7},{3,6},{4,1},{5,0},{6,3},{7,2}} | collective-permute-start | bytes 3145736 | tf_op jit(solution)/shard_map/ppermute | solution.py:447
  257.7 92.8 %all-to-all-start.1 = ((f32[8,32,512]{2,1,0:T(8,128)}), f32[8,32,512]{2,1,0:T(8,128)S(1)}, u32[]{:S(2)}, u32[]{:S(2)}) async-start(f32[8,32,512]{2,1,0:T(8,128)} %broadcast_in_dim.26), calls=%async_computation.1 | async-start | bytes 1048576 | tf_op jit(solution)/shard_map/all_to_all | solution.py:522
  259.9 97.7 %collective-permute-start.23 = (bf16[512,1024]{1,0:T(8,128)(2,1)}, bf16[512,1024]{1,0:T(8,128)(2,1)}, u32[]{:S(2)}, u32[]{:S(2)}) collective-permute-start(bf16[512,1024]{1,0:T(8,128)(2,1)} %add_convert_fusion.5), channel_id=1, source_target_pairs={{0,6},{1,7},{2,4},{3,5},{4,2},{5,3},{6,0},{7,1}} | collective-permute-start | bytes 3145736 | tf_op jit(solution)/shard_map/ppermute | solution.py:447
  262.8 99.6 %collective-permute-start.27 = (bf16[512,1024]{1,0:T(8,128)(2,1)}, bf16[512,1024]{1,0:T(8,128)(2,1)}, u32[]{:S(2)}, u32[]{:S(2)}) collective-permute-start(bf16[512,1024]{1,0:T(8,128)(2,1)} %add_convert_fusion.4), channel_id=1, source_target_pairs={{0,7},{1,6},{2,5},{3,4},{4,3},{5,2},{6,1},{7,0}} | collective-permute-start | bytes 3145736 | tf_op jit(solution)/shard_map/ppermute | solution.py:447
  277.8 79.0 %collective-permute-start.25 = (bf16[512,1024]{1,0:T(8,128)(2,1)}, bf16[512,1024]{1,0:T(8,128)(2,1)}, u32[]{:S(2)}, u32[]{:S(2)}) collective-permute-start(bf16[512,1024]{1,0:T(8,128)(2,1)} %get-tuple-element.170), channel_id=1, source_target_pairs={{0,3},{1,2},{2,1},{3,0},{4,7},{5,6},{6,5},{7,4}} | collective-permute-start | bytes 3145736 | tf_op jit(solution)/shard_map/ppermute | solution.py:447
  (32 other events, 458.1 us)
where the time goes:
time: 368 us; the launch traced here: 367 us
  Pallas kernels  196 us (53%)
  waiting for transfers between devices  103 us (28%)
  starting transfers between devices  27 us (7%)
  other arithmetic  26.1 us (7%)
  local copies, waits for them, and re-layouts  12.1 us (3%)
    pallas_call x4, Pallas kernels, run_chunk(): pl.pallas_call(functools.partial(chunk_kernel, first, toks), grid_spec=pl...  147 us
    ppermute x28, waiting for transfers between devices, flip(): lax.ppermute(arr, ('tp', 'ep'), [(s, s ^ turned) for s in range(n_dev)])  62 us
    pallas_call x2, Pallas kernels, run_wgrad(): pl.pallas_call(functools.partial(wgrad_kernel, n_c, first_e, len(prev)),...  41.6 us
    all_to_all x1, waiting for transfers between devices, device_fn(): lax.all_to_all(jnp.broadcast_to(d_logits[None], (n_dev, *d_logits.shape))...  41 us
    ppermute x28, starting transfers between devices, flip(): lax.ppermute(arr, ('tp', 'ep'), [(s, s ^ turned) for s in range(n_dev)])  22.4 us
    convert_element_type x5, other arithmetic, both(): add = lambda a, b: (a.astype(F32) + b.astype(F32)).astype(BF)  12.5 us
    convert_element_type x2, other arithmetic, device_fn(): return (moe.astype(BF), d_x.astype(BF), gw1, gb1, gw2, gb2, gwr, gbr)  9.17 us
  transfers between devices with their start and end apart: 30, of which 7 were waited for; matrix products, arithmetic and copies ran while one was open for 9% of the time, Pallas kernels for 53%

commit v1 on v0

--- a/solution.py
+++ b/solution.py
@@ -65,6 +65,8 @@
             for copy in reversed(loads[i]):
                 copy.start()
             off[i] = 0
+        sel[...] = jnp.zeros_like(sel)
+        zbuf[...] = jnp.zeros_like(zbuf)
 
     if first:
         w1_ref[0] = dot(w1_in[0], split_ref[...]).astype(BF)
@@ -118,7 +120,7 @@
             pos = lax.broadcasted_iota(jnp.int32, (m, toks), 0).astype(F32)
             hot = jnp.broadcast_to(rst[i, pl.ds(row, 1), :] - base, (m, toks)) == pos
             hot_b = jnp.where(hot, 1.0, 0.0).astype(BF)
-            sel[i, pl.ds(pl.multiple_of(off[i], 128), m), :] = hot_b
+            sel[i, pl.ds(pl.multiple_of(off[i], 16), m), :] = hot_b
             w_rows.append(jnp.sum(jnp.where(hot, jnp.broadcast_to(wst[i, pl.ds(row, 1), :], (m, toks)), 0.0), axis=1, keepdims=True))
             hots.append(hot)
             dst = pl.ds(pl.multiple_of(t * TILE + at, 128), m)
@@ -155,7 +157,7 @@
         def put(k, c, value):
             at = 0
             for i, m in parts:
-                zbuf[k, i, pl.ds(pl.multiple_of(off[i], 128), m), c] = value[at:at + m]
+                zbuf[k, i, pl.ds(pl.multiple_of(off[i], 16), m), c] = value[at:at + m]
                 at += m
 
         for c in cuts:
@@ -169,7 +171,8 @@
         for (i, m), hot in zip(parts, hots):
             dg = jnp.sum(jnp.where(hot, dg_row[at:at + m], 0.0), axis=0, keepdims=True)
             dg_ref[0, i:i + 1, :] += dg
-            off[i] = off[i] + m
+            used = jnp.clip(counts[i] - t * seg, 0, seg)
+            off[i] = off[i] + (used + 15) // 16 * 16
             at += m
 
         return 0
@@ -184,7 +187,7 @@
 
         def combine(j):
             i, k = j // 2, lax.rem(j, 2)
-            total = pl.multiple_of(off[i], 128)
+            total = off[i]
             acc[...] = dot(sel[i, :long, :], zbuf[k, i, :long, :], LHS)
 
             def step(q, _):
@@ -195,12 +198,6 @@
             lax.fori_loop(4, (total + TILE - 1) // TILE, step, 0)
             ost[i, k] = acc[...].astype(BF)
             return 0
-
-        for i in range(2):
-            total = pl.multiple_of(off[i], 128)
-            sel[i, pl.ds(total, TILE), :] = jnp.zeros((TILE, toks), BF)
-            for k in range(2):
-                zbuf[k, i, pl.ds(total, TILE), :] = jnp.zeros((TILE, dim), BF)
 
         def go(j, _):
             combine(j)
@@ -510,17 +507,15 @@
         slot_of = jnp.array([rel.index(m) for m in range(n_dev)], jnp.int32)
         dg_abs = dg_rel[slot_of[jnp.arange(n_dev) ^ me]]
         dg_back = lax.all_to_all(dg_abs, ('ep', 'tp'), 0, 0, tiled=True)
-        nt_all = jnp.stack(nts)
+        sum_3, nt_all = lax.optimization_barrier((both(3), jnp.stack(nts)))
+        got_3 = hop(3, *sum_3)
         unmix = split_mat.T
-        part_e = n_e // 4
+        part_e = n_e // 2
         grads = run_wgrad(nt_all, saved, unmix, 0, part_e, n_e)
-        last, dg_back, nt_b, grads = lax.optimization_barrier((part[3], dg_back, nt_all, grads))
-        part[3] = last
+        dg_back, nt_b, grads = lax.optimization_barrier((dg_back, nt_all, grads))
         d_gate = jnp.sum(dg_back.reshape(ep_count, tp_count, n_e, toks), axis=1).reshape(n_experts, toks)
         d_logits = w_full * (d_gate - jnp.sum(w_full * d_gate, axis=0, keepdims=True))
-        sum_3, d_logits, nt_b, grads = lax.optimization_barrier((both(3), d_logits, nt_b, grads))
         d_all = lax.all_to_all(jnp.broadcast_to(d_logits[None], (n_dev, *d_logits.shape)), ('ep', 'tp'), 0, 0, tiled=True)
-        got_3 = hop(3, *sum_3)
         gw1, gw2 = run_wgrad(nt_b, saved, unmix, part_e, n_e - part_e, n_e, grads)
         gb1 = functools.reduce(jnp.add, gb1s)[:, 0, :]
         gb1 = jnp.stack([gb1[:, :half], gb1[:, half:]], axis=2).reshape(n_e, wide)

time: 368 us -> 351 us (0.954)
  waiting for transfers between devices: 103 us -> 88.6 us
  Pallas kernels: 196 us -> 187 us
    all_to_all x1, waiting for transfers between devices: 41 us -> 0.01 us  [device_fn(): lax.all_to_all(jnp.broadcast_to(d_logits[None], (n_dev, *d_logits.shape))...]
    ppermute x28, waiting for transfers between devices: 62 us -> 88.6 us  [flip(): lax.ppermute(arr, ('tp', 'ep'), [(s, s ^ turned) for s in range(n_dev)])]
    pallas_call x4, Pallas kernels: 147 us -> 138 us  [run_chunk(): pl.pallas_call(functools.partial(chunk_kernel, first, toks), grid_spec=pl...]
    convert_element_type x5 -> x6, other arithmetic: 12.5 us -> 12 us  [both(): add = lambda a, b: (a.astype(F32) + b.astype(F32)).astype(BF)]
  transfers between devices with their start and end apart: 30 -> 30, of which waited for: 7 -> 4; matrix products, arithmetic and copies ran while one was open for 9% -> 9% of each run, Pallas kernels for 53% -> 53%
where the time goes in v1:
time: 351 us; the launch traced here: 350 us
  Pallas kernels  187 us (53%)
  waiting for transfers between devices  88.6 us (25%)
  starting transfers between devices  30.4 us (9%)
  other arithmetic  28 us (8%)
  local copies, waits for them, and re-layouts  13.2 us (4%)
    pallas_call x4, Pallas kernels, run_chunk(): pl.pallas_call(functools.partial(chunk_kernel, first, toks), grid_spec=pl...  138 us
    ppermute x28, waiting for transfers between devices, flip(): lax.ppermute(arr, ('tp', 'ep'), [(s, s ^ turned) for s in range(n_dev)])  88.6 us
    pallas_call x2, Pallas kernels, run_wgrad(): pl.pallas_call(functools.partial(wgrad_kernel, n_c, first_e, len(prev)),...  41.6 us
    ppermute x28, starting transfers between devices, flip(): lax.ppermute(arr, ('tp', 'ep'), [(s, s ^ turned) for s in range(n_dev)])  24.4 us
    convert_element_type x6, other arithmetic, both(): add = lambda a, b: (a.astype(F32) + b.astype(F32)).astype(BF)  12 us
    convert_element_type x2, other arithmetic, device_fn(): return (moe.astype(BF), d_x.astype(BF), gw1, gb1, gw2, gb2, gwr, gbr)  9.17 us
  transfers between devices with their start and end apart: 30, of which 4 were waited for; matrix products, arithmetic and copies ran while one was open for 9% of the time, Pallas kernels for 53%

profile of v1, /device:TPU:0, one launch (start us, length us, event | category | flops | bytes accessed | tf_op | source)
XLA Modules:
  0.0 350.1 jit_solution(9183563656675486309)
XLA Ops:
  4.9 1.9 pack.1
  6.8 2.8 collective-permute-start.3
  15.7 43.0 %collective-permute-done.2.xa_hbm.refs_2_ = bf16[512,1024]{1,0:T(8,128)(2,1)} collective-permute-done((bf16[512,1024]{1,0:T(8,128)(2,1)}, bf16[512,1024]{1,0:T(8,128)(2,1)}, u32[]{:S(2)}, u32[]{:S(2)}) %collective-permute-start.2) | collective-permute-done | bytes 1048608 | tf_op jit(solution)/shard_map/ppermute | solution.py:444
  58.7 2.4 collective-permute-start.9
  63.7 37.4 %experts.4 = (bf16[512,1024]{1,0:T(8,128)(2,1)}, bf16[512,1024]{1,0:T(8,128)(2,1)}, bf16[512,1024]{1,0:T(8,128)(2,1)}, bf16[512,1024]{1,0:T(8,128)(2,1)}, f32[8,...) custom-call(s32[1]{0:T(128)} %bitcast.4.ep_ref, ...), custom_call_target="tpu_custom_call" | custom-call | flops 28000000000 | bytes 40000000 | tf_op jit(solution)/shard_map/experts/pallas_call | solution.py:253
  101.1 31.8 %experts.5 = (bf16[512,1024]{1,0:T(8,128)(2,1)}, bf16[512,1024]{1,0:T(8,128)(2,1)}, bf16[512,1024]{1,0:T(8,128)(2,1)}, bf16[512,1024]{1,0:T(8,128)(2,1)}, f32[8,...) custom-call(s32[1]{0:T(128)} %bitcast.4.ep_ref, ...), custom_call_target="tpu_custom_call" | custom-call | flops 28000000000 | bytes 40000000 | tf_op jit(solution)/shard_map/experts/pallas_call | solution.py:253
  134.1 3.8 %collective-permute-start.15 = (bf16[576,1024]{1,0:T(8,128)(2,1)}, bf16[576,1024]{1,0:T(8,128)(2,1)}, u32[]{:S(2)}, u32[]{:S(2)}) collective-permute-start(bf16[576,1024]{1,0:T(8,128)(2,1)} %copy-done.5), channel_id=1, source_target_pairs={{0,3},{1,2},{2,1},{3,0},{4,7},{5,6},{6,5},{7,4}} | collective-permute-start | bytes 3538952 | tf_op jit(solution)/shard_map/ppermute | solution.py:444
  137.9 2.6 add_convert_fusion.7
  142.1 34.9 %experts.6 = (bf16[512,1024]{1,0:T(8,128)(2,1)}, bf16[512,1024]{1,0:T(8,128)(2,1)}, bf16[512,1024]{1,0:T(8,128)(2,1)}, bf16[512,1024]{1,0:T(8,128)(2,1)}, f32[8,...) custom-call(s32[1]{0:T(128)} %bitcast.4.ep_ref, ...), custom_call_target="tpu_custom_call" | custom-call | flops 28000000000 | bytes 40000000 | tf_op jit(solution)/shard_map/experts/pallas_call | solution.py:253
  180.2 2.6 add_convert_fusion.5
  184.2 2.0 collective-permute-done.16.da_hbm
  186.2 33.8 %experts.7 = (bf16[512,1024]{1,0:T(8,128)(2,1)}, bf16[512,1024]{1,0:T(8,128)(2,1)}, bf16[512,1024]{1,0:T(8,128)(2,1)}, bf16[512,1024]{1,0:T(8,128)(2,1)}, f32[8,...) custom-call(s32[1]{0:T(128)} %bitcast.4.ep_ref, ...), custom_call_target="tpu_custom_call" | custom-call | flops 28000000000 | bytes 40000000 | tf_op jit(solution)/shard_map/experts/pallas_call | solution.py:253
  223.7 3.8 %all-to-all-start = ((f32[8,8,512]{2,1,0:T(8,128)}), f32[8,8,512]{2,1,0:T(8,128)}, u32[]{:S(2)}, u32[]{:S(2)}) async-start(f32[8,8,512]{2,1,0:T(8,128)} %gather_fusion.1), calls=%async_computation | async-start | bytes 262144 | tf_op jit(solution)/shard_map/all_to_all | solution.py:509
  231.0 1.7 collective-permute-start.26
  232.8 2.6 add_convert_fusion.3
  238.2 22.0 %weight_grads.2 = (bf16[8,1024,512]{2,1,0:T(8,128)(2,1)}, bf16[8,256,1024]{2,1,0:T(8,128)(2,1)}) custom-call(s32[4,8]{1,0:T(4,128)} %pad_add_fusion.nt_ref, bf16[8,2,256,1024]{3,2,1,0:T(8,128)(2,1)} %get-tuple-element.123.refs_0_, bf16[8,2,256,1024]{3,2,1,0:T(8,128)(2,1)} %get-tuple-element.124.refs_1_, ...), custom_call_target="tpu_custom_call" | custom-call | flops 25999998976 | bytes 60000000 | tf_op jit(solution)/shard_map/weight_grads/pallas_call | solution.py:342
  262.1 2.2 all-to-all-start.1
  264.4 2.9 collective-permute-start.23
  269.0 19.6 %weight_grads.3 = (bf16[8,1024,512]{2,1,0:T(8,128)(2,1)}, bf16[8,256,1024]{2,1,0:T(8,128)(2,1)}) custom-call(s32[4,8]{1,0:T(4,128)} %pad_add_fusion.nt_ref, bf16[8,2,256,1024]{3,2,1,0:T(8,128)(2,1)} %get-tuple-element.123.refs_0_, bf16[8,2,256,1024]{3,2,1,0:T(8,128)(2,1)} %get-tuple-element.124.refs_1_, ...), custom_call_target="tpu_custom_call", output_to_operand_aliasing={{0}: (18, {}), {1}: (19, {})} | custom-call | flops 25999998976 | bytes 60000000 | tf_op jit(solution)/shard_map/weight_grads/pallas_call | solution.py:342
  288.6 1.8 fusion.4
  291.0 5.6 %router_grad.1 = f32[1024,32]{1,0:T(8,128)S(1)} custom-call(s32[1]{0:T(128)} %bitcast.22.me_ref, bf16[512,1024]{1,0:T(8,128)(2,1)} %refs_0_.1, bf16[512,1024]{1,0:T(8,128)(2,1)} %collective-permute-done.xb_hbm.refs_1_, bf16[512,1024]{1,0:T(8,128)(2,1)} %collective-permute-done.2.xa_hbm.refs_2_, bf16[512,1024]{1,0:T(8,128)(2,1)} %collective-permute-done.5.xb_hbm.refs_3_, ...), custom_call_target="tpu_custom_call" | custom-call | tf_op jit(solution)/shard_map/router_grad/pallas_call | solution.py:418
  296.6 43.4 %collective-permute-done.25 = bf16[512,1024]{1,0:T(8,128)(2,1)} collective-permute-done((bf16[512,1024]{1,0:T(8,128)(2,1)}, bf16[512,1024]{1,0:T(8,128)(2,1)}, u32[]{:S(2)}, u32[]{:S(2)}) %collective-permute-start.25) | collective-permute-done | bytes 1048608 | tf_op jit(solution)/shard_map/ppermute | solution.py:444
  340.9 4.8 %add_convert_fusion.1 = bf16[512,1024]{1,0:T(8,128)(2,1)} fusion(bf16[512,1024]{1,0:T(8,128)(2,1)} %collective-permute-done.24, bf16[512,1024]{1,0:T(8,128)(2,1)} %collective-permute-done.23, bf16[512,1024]{1,0:T(8,128)(2,1)} %collective-permute-done.22, bf16[512,1024]{1,0:T(8,128)(2,1)} %collective-permute-done.20, bf16[512,1024]{1,0:T(8,128)(2,1)} %get-tuple-element.150), kind=kLoop, calls=%fused_computation.3 | loop fusion | flops 5242880 | bytes 6291456 | tf_op jit(solution)/shard_map/convert_element_type | solution.py:532
  345.7 4.4 %add_convert_fusion = bf16[512,1024]{1,0:T(8,128)(2,1)} fusion(f32[512,1024]{1,0:T(8,128)S(1)} %copy-done.7, bf16[512,1024]{1,0:T(8,128)(2,1)} %collective-permute-done.25, bf16[512,1024]{1,0:T(8,128)(2,1)} %collective-permute-done.27, bf16[512,1024]{1,0:T(8,128)(2,1)} %collective-permute-done.26, bf16[512,1024]{1,0:T(8,128)(2,1)} %collective-permute-done.21, ...), kind=kLoop, calls=%fused_computation.2 | loop fusion | flops 5767168 | bytes 8388608 | tf_op jit(solution)/shard_map/convert_element_type | solution.py:532
  (133 shorter events, 35.2 us)
Async XLA Ops:
  6.8 54.3 %collective-permute-start.3 = (bf16[576,1024]{1,0:T(8,128)(2,1)S(1)}, bf16[576,1024]{1,0:T(8,128)(2,1)}, u32[]{:S(2)}, u32[]{:S(2)}) collective-permute-start(bf16[576,1024]{1,0:T(8,128)(2,1)S(1)} %get-tuple-element.92.da_hbm), channel_id=1, source_target_pairs={{0,5},{1,4},{2,7},{3,6},{4,1},{5,0},{6,3},{7,2}} | collective-permute-start | bytes 3538952 | tf_op jit(solution)/shard_map/ppermute | solution.py:444
  9.6 53.0 %collective-permute-start.1 = (bf16[576,1024]{1,0:T(8,128)(2,1)S(1)}, bf16[576,1024]{1,0:T(8,128)(2,1)S(1)}, u32[]{:S(2)}, u32[]{:S(2)}) collective-permute-start(bf16[576,1024]{1,0:T(8,128)(2,1)S(1)} %get-tuple-element.92.da_hbm), channel_id=1, source_target_pairs={{0,1},{1,0},{2,3},{3,2},{4,5},{5,4},{6,7},{7,6}} | collective-permute-start | bytes 3538952 | tf_op jit(solution)/shard_map/ppermute | solution.py:444
  10.3 48.4 %collective-permute-start.2 = (bf16[512,1024]{1,0:T(8,128)(2,1)}, bf16[512,1024]{1,0:T(8,128)(2,1)}, u32[]{:S(2)}, u32[]{:S(2)}) collective-permute-start(bf16[512,1024]{1,0:T(8,128)(2,1)} %refs_0_.1), channel_id=1, source_target_pairs={{0,4},{1,5},{2,6},{3,7},{4,0},{5,1},{6,2},{7,3}} | collective-permute-start | bytes 3145736 | tf_op jit(solution)/shard_map/ppermute | solution.py:444
  11.2 47.6 %collective-permute-start.8 = (bf16[512,1024]{1,0:T(8,128)(2,1)}, bf16[512,1024]{1,0:T(8,128)(2,1)}, u32[]{:S(2)}, u32[]{:S(2)}) collective-permute-start(bf16[512,1024]{1,0:T(8,128)(2,1)} %refs_0_.1), channel_id=1, source_target_pairs={{0,2},{1,3},{2,0},{3,1},{4,6},{5,7},{6,4},{7,5}} | collective-permute-start | bytes 3145736 | tf_op jit(solution)/shard_map/ppermute | solution.py:444
  12.6 50.0 %collective-permute-start = (bf16[512,1024]{1,0:T(8,128)(2,1)}, bf16[512,1024]{1,0:T(8,128)(2,1)}, u32[]{:S(2)}, u32[]{:S(2)}) collective-permute-start(bf16[512,1024]{1,0:T(8,128)(2,1)} %refs_0_.1), channel_id=1, source_target_pairs={{0,1},{1,0},{2,3},{3,2},{4,5},{5,4},{6,7},{7,6}} | collective-permute-start | bytes 3145736 | tf_op jit(solution)/shard_map/ppermute | solution.py:444
  58.7 42.4 %collective-permute-start.5 = (bf16[512,1024]{1,0:T(8,128)(2,1)}, bf16[512,1024]{1,0:T(8,128)(2,1)}, u32[]{:S(2)}, u32[]{:S(2)}) collective-permute-start(bf16[512,1024]{1,0:T(8,128)(2,1)} %collective-permute-done.2.xa_hbm.refs_2_), channel_id=1, source_target_pairs={{0,1},{1,0},{2,3},{3,2},{4,5},{5,4},{6,7},{7,6}} | collective-permute-start | bytes 3145736 | tf_op jit(solution)/shard_map/ppermute | solution.py:444
  58.7 75.3 %collective-permute-start.9 = (bf16[512,1024]{1,0:T(8,128)(2,1)}, bf16[512,1024]{1,0:T(8,128)(2,1)}, u32[]{:S(2)}, u32[]{:S(2)}) collective-permute-start(bf16[512,1024]{1,0:T(8,128)(2,1)} %collective-permute-done.8.xa_hbm.refs_6_), channel_id=1, source_target_pairs={{0,4},{1,5},{2,6},{3,7},{4,0},{5,1},{6,2},{7,3}} | collective-permute-start | bytes 3145736 | tf_op jit(solution)/shard_map/ppermute | solution.py:444
  61.1 72.4 %collective-permute-start.10 = (bf16[576,1024]{1,0:T(8,128)(2,1)}, bf16[576,1024]{1,0:T(8,128)(2,1)}, u32[]{:S(2)}, u32[]{:S(2)}) collective-permute-start(bf16[576,1024]{1,0:T(8,128)(2,1)} %collective-permute-done.3.db_hbm), channel_id=1, source_target_pairs={{0,2},{1,3},{2,0},{3,1},{4,6},{5,7},{6,4},{7,5}} | collective-permute-start | bytes 3538952 | tf_op jit(solution)/shard_map/ppermute | solution.py:444
  62.6 38.5 %collective-permute-start.4 = (bf16[576,1024]{1,0:T(8,128)(2,1)}, bf16[576,1024]{1,0:T(8,128)(2,1)}, u32[]{:S(2)}, u32[]{:S(2)}) collective-permute-start(bf16[576,1024]{1,0:T(8,128)(2,1)} %collective-permute-done.3.db_hbm), channel_id=1, source_target_pairs={{0,1},{1,0},{2,3},{3,2},{4,5},{5,4},{6,7},{7,6}} | collective-permute-start | bytes 3538952 | tf_op jit(solution)/shard_map/ppermute | solution.py:444
  133.5 8.5 %collective-permute-start.11 = (bf16[576,1024]{1,0:T(8,128)(2,1)}, bf16[576,1024]{1,0:T(8,128)(2,1)}, u32[]{:S(2)}, u32[]{:S(2)}) collective-permute-start(bf16[576,1024]{1,0:T(8,128)(2,1)} %collective-permute-done.10.db_hbm), channel_id=1, source_target_pairs={{0,1},{1,0},{2,3},{3,2},{4,5},{5,4},{6,7},{7,6}} | collective-permute-start | bytes 3538952 | tf_op jit(solution)/shard_map/ppermute | solution.py:444
  134.0 8.0 %collective-permute-start.12 = (bf16[512,1024]{1,0:T(8,128)(2,1)}, bf16[512,1024]{1,0:T(8,128)(2,1)}, u32[]{:S(2)}, u32[]{:S(2)}) collective-permute-start(bf16[512,1024]{1,0:T(8,128)(2,1)} %collective-permute-done.9.xa_hbm.refs_4_), channel_id=1, source_target_pairs={{0,1},{1,0},{2,3},{3,2},{4,5},{5,4},{6,7},{7,6}} | collective-permute-start | bytes 3145736 | tf_op jit(solution)/shard_map/ppermute | solution.py:444
  134.1 44.7 %collective-permute-start.15 = (bf16[576,1024]{1,0:T(8,128)(2,1)}, bf16[576,1024]{1,0:T(8,128)(2,1)}, u32[]{:S(2)}, u32[]{:S(2)}) collective-permute-start(bf16[576,1024]{1,0:T(8,128)(2,1)} %copy-done.5), channel_id=1, source_target_pairs={{0,3},{1,2},{2,1},{3,0},{4,7},{5,6},{6,5},{7,4}} | collective-permute-start | bytes 3538952 | tf_op jit(solution)/shard_map/ppermute | solution.py:444
  178.2 86.1 %collective-permute-start.20 = (bf16[512,1024]{1,0:T(8,128)(2,1)}, bf16[512,1024]{1,0:T(8,128)(2,1)}, u32[]{:S(2)}, u32[]{:S(2)}) collective-permute-start(bf16[512,1024]{1,0:T(8,128)(2,1)} %get-tuple-element.147), channel_id=1, source_target_pairs={{0,1},{1,0},{2,3},{3,2},{4,5},{5,4},{6,7},{7,6}} | collective-permute-start | bytes 3145736 | tf_op jit(solution)/shard_map/ppermute | solution.py:444
  179.9 87.4 %collective-permute-start.21 = (bf16[512,1024]{1,0:T(8,128)(2,1)}, bf16[512,1024]{1,0:T(8,128)(2,1)}, u32[]{:S(2)}, u32[]{:S(2)}) collective-permute-start(bf16[512,1024]{1,0:T(8,128)(2,1)} %get-tuple-element.149), channel_id=1, source_target_pairs={{0,1},{1,0},{2,3},{3,2},{4,5},{5,4},{6,7},{7,6}} | collective-permute-start | bytes 3145736 | tf_op jit(solution)/shard_map/ppermute | solution.py:444
  182.8 158.1 %collective-permute-start.22 = (bf16[512,1024]{1,0:T(8,128)(2,1)}, bf16[512,1024]{1,0:T(8,128)(2,1)}, u32[]{:S(2)}, u32[]{:S(2)}) collective-permute-start(bf16[512,1024]{1,0:T(8,128)(2,1)} %add_convert_fusion.7), channel_id=1, source_target_pairs={{0,4},{1,5},{2,6},{3,7},{4,0},{5,1},{6,2},{7,3}} | collective-permute-start | bytes 3145736 | tf_op jit(solution)/shard_map/ppermute | solution.py:444
  220.0 11.0 %collective-permute-start.18 = (bf16[512,1024]{1,0:T(8,128)(2,1)}, bf16[512,1024]{1,0:T(8,128)(2,1)}, u32[]{:S(2)}, u32[]{:S(2)}) collective-permute-start(bf16[512,1024]{1,0:T(8,128)(2,1)} %get-tuple-element.115), channel_id=1, source_target_pairs={{0,1},{1,0},{2,3},{3,2},{4,5},{5,4},{6,7},{7,6}} | collective-permute-start | bytes 3145736 | tf_op jit(solution)/shard_map/ppermute | solution.py:444
  220.0 15.3 %collective-permute-start.19 = (bf16[512,1024]{1,0:T(8,128)(2,1)}, bf16[512,1024]{1,0:T(8,128)(2,1)S(1)}, u32[]{:S(2)}, u32[]{:S(2)}) collective-permute-start(bf16[512,1024]{1,0:T(8,128)(2,1)} %get-tuple-element.117), channel_id=1, source_target_pairs={{0,1},{1,0},{2,3},{3,2},{4,5},{5,4},{6,7},{7,6}} | collective-permute-start | bytes 3145736 | tf_op jit(solution)/shard_map/ppermute | solution.py:444
  223.7 36.6 %all-to-all-start = ((f32[8,8,512]{2,1,0:T(8,128)}), f32[8,8,512]{2,1,0:T(8,128)}, u32[]{:S(2)}, u32[]{:S(2)}) async-start(f32[8,8,512]{2,1,0:T(8,128)} %gather_fusion.1), calls=%async_computation | async-start | bytes 262144 | tf_op jit(solution)/shard_map/all_to_all | solution.py:509
  231.0 114.6 %collective-permute-start.26 = (bf16[512,1024]{1,0:T(8,128)(2,1)}, bf16[512,1024]{1,0:T(8,128)(2,1)}, u32[]{:S(2)}, u32[]{:S(2)}) collective-permute-start(bf16[512,1024]{1,0:T(8,128)(2,1)} %add_convert_fusion.6), channel_id=1, source_target_pairs={{0,5},{1,4},{2,7},{3,6},{4,1},{5,0},{6,3},{7,2}} | collective-permute-start | bytes 3145736 | tf_op jit(solution)/shard_map/ppermute | solution.py:444
  236.8 30.5 %collective-permute-start.24 = (bf16[512,1024]{1,0:T(8,128)(2,1)}, bf16[512,1024]{1,0:T(8,128)(2,1)}, u32[]{:S(2)}, u32[]{:S(2)}) collective-permute-start(bf16[512,1024]{1,0:T(8,128)(2,1)} %add_convert_fusion.3), channel_id=1, source_target_pairs={{0,2},{1,3},{2,0},{3,1},{4,6},{5,7},{6,4},{7,5}} | collective-permute-start | bytes 3145736 | tf_op jit(solution)/shard_map/ppermute | solution.py:444
  262.1 28.2 %all-to-all-start.1 = ((f32[8,32,512]{2,1,0:T(8,128)}), f32[8,32,512]{2,1,0:T(8,128)S(1)}, u32[]{:S(2)}, u32[]{:S(2)}) async-start(f32[8,32,512]{2,1,0:T(8,128)} %broadcast_in_dim.26), calls=%async_computation.1 | async-start | bytes 1048576 | tf_op jit(solution)/shard_map/all_to_all | solution.py:518
  264.4 76.5 %collective-permute-start.23 = (bf16[512,1024]{1,0:T(8,128)(2,1)}, bf16[512,1024]{1,0:T(8,128)(2,1)}, u32[]{:S(2)}, u32[]{:S(2)}) collective-permute-start(bf16[512,1024]{1,0:T(8,128)(2,1)} %add_convert_fusion.5), channel_id=1, source_target_pairs={{0,6},{1,7},{2,4},{3,5},{4,2},{5,3},{6,0},{7,1}} | collective-permute-start | bytes 3145736 | tf_op jit(solution)/shard_map/ppermute | solution.py:444
  267.2 78.4 %collective-permute-start.27 = (bf16[512,1024]{1,0:T(8,128)(2,1)}, bf16[512,1024]{1,0:T(8,128)(2,1)}, u32[]{:S(2)}, u32[]{:S(2)}) collective-permute-start(bf16[512,1024]{1,0:T(8,128)(2,1)} %add_convert_fusion.4), channel_id=1, source_target_pairs={{0,7},{1,6},{2,5},{3,4},{4,3},{5,2},{6,1},{7,0}} | collective-permute-start | bytes 3145736 | tf_op jit(solution)/shard_map/ppermute | solution.py:444
  267.3 72.8 %collective-permute-start.25 = (bf16[512,1024]{1,0:T(8,128)(2,1)}, bf16[512,1024]{1,0:T(8,128)(2,1)}, u32[]{:S(2)}, u32[]{:S(2)}) collective-permute-start(bf16[512,1024]{1,0:T(8,128)(2,1)} %add_convert_fusion.2), channel_id=1, source_target_pairs={{0,3},{1,2},{2,1},{3,0},{4,7},{5,6},{6,5},{7,4}} | collective-permute-start | bytes 3145736 | tf_op jit(solution)/shard_map/ppermute | solution.py:444
  (29 other events, 442.2 us)

commit v2 on v1

--- a/solution.py
+++ b/solution.py
@@ -284,22 +284,22 @@
     return got[:4], got[4:8], got[-4:], (got[8] if first else w1)
 
 
-def wgrad_kernel(n_c, first_e, n_prev, nt_ref, *refs):
+def wgrad_kernel(n_c, *refs):
+    nts, refs = refs[:n_c], refs[n_c:]
     hbm = [refs[k * n_c:(k + 1) * n_c] for k in range(4)]
-    mix_ref = refs[4 * n_c]
-    gw1_ref, gw2_ref, acc1, acc2, *bufs, sems = refs[4 * n_c + 1 + n_prev:]
+    mix_ref, gw1_ref, gw2_ref, nt_ref, acc1, acc2, *bufs, sems = refs[4 * n_c:]
     e = pl.program_id(0)
     n_e = pl.num_programs(0)
     par = lax.rem(e, 2)
 
     def fetches(step, c, t, p):
-        return [pltpu.make_async_copy(hbm[k][c].at[first_e + step, t], bufs[k].at[p, 2 * c + t], sems.at[p, 2 * c + t, k])
+        return [pltpu.make_async_copy(hbm[k][c].at[step, t], bufs[k].at[p, 2 * c + t], sems.at[p, 2 * c + t, k])
                 for k in range(4)]
 
     def each(step, act):
         for c in range(n_c):
             for t in range(2):
-                pl.when(nt_ref[c, first_e + step] > t)(functools.partial(act, c, t))
+                pl.when(nt_ref[c, step] > t)(functools.partial(act, c, t))
 
     def start(step, p):
         def go(c, t):
@@ -310,6 +310,9 @@
 
     @pl.when(e == 0)
     def _():
+        for c in range(n_c):
+            for k in range(nts[c].shape[0]):
+                nt_ref[c, k] = nts[c][k]
         start(e, par)
 
     @pl.when(e + 1 < n_e)
@@ -320,7 +323,7 @@
     acc2[...] = jnp.zeros_like(acc2)
 
     def add(j, _):
-        @pl.when(nt_ref[j // 2, first_e + e] > lax.rem(j, 2))
+        @pl.when(nt_ref[j // 2, e] > lax.rem(j, 2))
         def _():
             for k in range(4):
                 pltpu.make_async_copy(hbm[k][0].at[0, 0], bufs[k].at[par, j], sems.at[par, j, k]).wait()
@@ -335,28 +338,27 @@
     gw1_ref[0] = dot(acc1[...].astype(BF), mix_ref[...]).astype(BF)
 
 
-def run_wgrad(nt, saved, unmix, first_e, n_e, all_e, prev=()):
+def run_wgrad(nts, saved, unmix):
     n_c = len(saved)
     xs, ds, dh, wa = (list(t) for t in zip(*saved))
-    dim, wide, half = xs[0].shape[3], dh[0].shape[3], wa[0].shape[3]
+    n_e, dim, wide, half = xs[0].shape[0], xs[0].shape[3], dh[0].shape[3], wa[0].shape[3]
+    per_e = lambda e, *nts: (e, 0, 0)
     return pl.pallas_call(
-        functools.partial(wgrad_kernel, n_c, first_e, len(prev)),
+        functools.partial(wgrad_kernel, n_c),
         grid_spec=pltpu.PrefetchScalarGridSpec(
-            num_scalar_prefetch=1,
+            num_scalar_prefetch=n_c,
             grid=(n_e,),
-            in_specs=[pl.BlockSpec(memory_space=pl.ANY)] * (4 * n_c) + [pl.BlockSpec((wide, wide), lambda e, nt: (0, 0))]
-            + [pl.BlockSpec(memory_space=pl.ANY)] * len(prev),
-            out_specs=[pl.BlockSpec((1, dim, wide), lambda e, nt: (first_e + e, 0, 0)), pl.BlockSpec((1, half, dim), lambda e, nt: (first_e + e, 0, 0))],
-            scratch_shapes=[pltpu.VMEM((dim, wide), F32), pltpu.VMEM((half, dim), F32)]
+            in_specs=[pl.BlockSpec(memory_space=pl.ANY)] * (4 * n_c) + [pl.BlockSpec((wide, wide), lambda e, *nts: (0, 0))],
+            out_specs=[pl.BlockSpec((1, dim, wide), per_e), pl.BlockSpec((1, half, dim), per_e)],
+            scratch_shapes=[pltpu.SMEM((n_c, n_e), jnp.int32), pltpu.VMEM((dim, wide), F32), pltpu.VMEM((half, dim), F32)]
             + [pltpu.VMEM((2, 2 * n_c, TILE, w), BF) for w in (dim, dim, wide, half)]
             + [pltpu.SemaphoreType.DMA((2, 2 * n_c, 4))],
         ),
-        out_shape=[jax.ShapeDtypeStruct((all_e, dim, wide), BF), jax.ShapeDtypeStruct((all_e, half, dim), BF)],
-        input_output_aliases={4 * n_c + 2 + k: k for k in range(len(prev))},
+        out_shape=[jax.ShapeDtypeStruct((n_e, dim, wide), BF), jax.ShapeDtypeStruct((n_e, half, dim), BF)],
         compiler_params=pltpu.CompilerParams(dimension_semantics=('arbitrary',), vmem_limit_bytes=64000 * 1024),
         cost_estimate=pl.CostEstimate(flops=26_000_000_000, bytes_accessed=60_000_000, transcendentals=0),
         name='weight_grads',
-    )(nt, *xs, *ds, *dh, *wa, unmix, *prev)
+    )(*nts, *xs, *ds, *dh, *wa, unmix)
 
 
 def pack_kernel(x_ref, d_ref, idx_ref, slot_ref, wr_ref, br_ref, tall_ref, w_ref):
@@ -507,16 +509,12 @@
         slot_of = jnp.array([rel.index(m) for m in range(n_dev)], jnp.int32)
         dg_abs = dg_rel[slot_of[jnp.arange(n_dev) ^ me]]
         dg_back = lax.all_to_all(dg_abs, ('ep', 'tp'), 0, 0, tiled=True)
-        sum_3, nt_all = lax.optimization_barrier((both(3), jnp.stack(nts)))
-        got_3 = hop(3, *sum_3)
-        unmix = split_mat.T
-        part_e = n_e // 2
-        grads = run_wgrad(nt_all, saved, unmix, 0, part_e, n_e)
-        dg_back, nt_b, grads = lax.optimization_barrier((dg_back, nt_all, grads))
         d_gate = jnp.sum(dg_back.reshape(ep_count, tp_count, n_e, toks), axis=1).reshape(n_experts, toks)
         d_logits = w_full * (d_gate - jnp.sum(w_full * d_gate, axis=0, keepdims=True))
+        sum_3, d_logits, last = lax.optimization_barrier((both(3), d_logits, saved[3]))
         d_all = lax.all_to_all(jnp.broadcast_to(d_logits[None], (n_dev, *d_logits.shape)), ('ep', 'tp'), 0, 0, tiled=True)
-        gw1, gw2 = run_wgrad(nt_b, saved, unmix, part_e, n_e - part_e, n_e, grads)
+        got_3 = hop(3, *sum_3)
+        gw1, gw2 = run_wgrad(nts, [*saved[:3], last], split_mat.T)
         gb1 = functools.reduce(jnp.add, gb1s)[:, 0, :]
         gb1 = jnp.stack([gb1[:, :half], gb1[:, half:]], axis=2).reshape(n_e, wide)
         gb2 = functools.reduce(jnp.add, gb2s)

time: 351 us -> 351 us (level)
  waiting for transfers between devices: 88.6 us -> 97.9 us
  Pallas kernels: 187 us -> 183 us
    all_to_all x1, waiting for transfers between devices: 0.01 us -> 33 us  [device_fn(): lax.all_to_all(jnp.broadcast_to(d_logits[None], (n_dev, *d_logits.shape))...]
    ppermute x28, waiting for transfers between devices: 88.6 us -> 60.5 us  [flip(): lax.ppermute(arr, ('tp', 'ep'), [(s, s ^ turned) for s in range(n_dev)])]
    all_to_all x1, waiting for transfers between devices: 0.01 us -> 4.46 us  [device_fn(): dg_back = lax.all_to_all(dg_abs, ('ep', 'tp'), 0, 0, tiled=True)]
    pallas_call x2 -> x1, Pallas kernels: 41.6 us -> 37.3 us  [run_wgrad(): pl.pallas_call(functools.partial(wgrad_kernel, n_c), grid_spec=pltpu.Pref...]
    unnamed x49 -> x59, local copies, waits for them, and re-layouts: 6.22 us -> 7.11 us
  transfers between devices with their start and end apart: 30 -> 30, of which waited for: 4 -> 5; matrix products, arithmetic and copies ran while one was open for 9% -> 9% of each run, Pallas kernels for 53% -> 42%
where the time goes in v2:
time: 351 us; the launch traced here: 350 us
  Pallas kernels  183 us (52%)
  waiting for transfers between devices  97.9 us (28%)
  starting transfers between devices  28 us (8%)
  other arithmetic  25.6 us (7%)
  local copies, waits for them, and re-layouts  13.3 us (4%)
    pallas_call x4, Pallas kernels, run_chunk(): pl.pallas_call(functools.partial(chunk_kernel, first, toks), grid_spec=pl...  138 us
    ppermute x28, waiting for transfers between devices, flip(): lax.ppermute(arr, ('tp', 'ep'), [(s, s ^ turned) for s in range(n_dev)])  60.5 us
    pallas_call x1, Pallas kernels, run_wgrad(): pl.pallas_call(functools.partial(wgrad_kernel, n_c), grid_spec=pltpu.Pref...  37.3 us
    all_to_all x1, waiting for transfers between devices, device_fn(): lax.all_to_all(jnp.broadcast_to(d_logits[None], (n_dev, *d_logits.shape))...  33 us
    ppermute x28, starting transfers between devices, flip(): lax.ppermute(arr, ('tp', 'ep'), [(s, s ^ turned) for s in range(n_dev)])  22.1 us
    convert_element_type x6, other arithmetic, both(): add = lambda a, b: (a.astype(F32) + b.astype(F32)).astype(BF)  13.3 us
    convert_element_type x2, other arithmetic, device_fn(): return (moe.astype(BF), d_x.astype(BF), gw1, gb1, gw2, gb2, gwr, gbr)  9.17 us
    unnamed x59, local copies, waits for them, and re-layouts  7.11 us
  transfers between devices with their start and end apart: 30, of which 5 were waited for; matrix products, arithmetic and copies ran while one was open for 9% of the time, Pallas kernels for 42%

profile of v2, /device:TPU:0, one launch (start us, length us, event | category | flops | bytes accessed | tf_op | source)
XLA Modules:
  0.0 350.5 jit_solution(1349721356527712159)
XLA Ops:
  4.9 1.9 pack.1
  6.8 2.8 collective-permute-start.1
  15.7 43.0 %collective-permute-done.xa_hbm.refs_2_ = bf16[512,1024]{1,0:T(8,128)(2,1)} collective-permute-done((bf16[512,1024]{1,0:T(8,128)(2,1)}, bf16[512,1024]{1,0:T(8,128)(2,1)}, u32[]{:S(2)}, u32[]{:S(2)}) %collective-permute-start) | collective-permute-done | bytes 1048608 | tf_op jit(solution)/shard_map/ppermute | solution.py:446
  58.7 2.4 collective-permute-start.9
  63.8 37.3 %experts.4 = (bf16[512,1024]{1,0:T(8,128)(2,1)}, bf16[512,1024]{1,0:T(8,128)(2,1)}, bf16[512,1024]{1,0:T(8,128)(2,1)}, bf16[512,1024]{1,0:T(8,128)(2,1)}, f32[8,...) custom-call(s32[1]{0:T(128)} %bitcast.ep_ref, ...), custom_call_target="tpu_custom_call" | custom-call | flops 28000000000 | bytes 40000000 | tf_op jit(solution)/shard_map/experts/pallas_call | solution.py:253
  101.1 31.9 %experts.5 = (bf16[512,1024]{1,0:T(8,128)(2,1)}, bf16[512,1024]{1,0:T(8,128)(2,1)}, bf16[512,1024]{1,0:T(8,128)(2,1)}, bf16[512,1024]{1,0:T(8,128)(2,1)}, f32[8,...) custom-call(s32[1]{0:T(128)} %bitcast.ep_ref, ...), custom_call_target="tpu_custom_call" | custom-call | flops 28000000000 | bytes 40000000 | tf_op jit(solution)/shard_map/experts/pallas_call | solution.py:253
  134.1 3.9 %collective-permute-start.15 = (bf16[576,1024]{1,0:T(8,128)(2,1)}, bf16[576,1024]{1,0:T(8,128)(2,1)}, u32[]{:S(2)}, u32[]{:S(2)}) collective-permute-start(bf16[576,1024]{1,0:T(8,128)(2,1)} %copy-done.5), channel_id=1, source_target_pairs={{0,3},{1,2},{2,1},{3,0},{4,7},{5,6},{6,5},{7,4}} | collective-permute-start | bytes 3538952 | tf_op jit(solution)/shard_map/ppermute | solution.py:446
  138.0 2.6 add_convert_fusion.6
  142.0 34.9 %experts.6 = (bf16[512,1024]{1,0:T(8,128)(2,1)}, bf16[512,1024]{1,0:T(8,128)(2,1)}, bf16[512,1024]{1,0:T(8,128)(2,1)}, bf16[512,1024]{1,0:T(8,128)(2,1)}, f32[8,...) custom-call(s32[1]{0:T(128)} %bitcast.ep_ref, ...), custom_call_target="tpu_custom_call" | custom-call | flops 28000000000 | bytes 40000000 | tf_op jit(solution)/shard_map/experts/pallas_call | solution.py:253
  179.8 2.7 add_convert_fusion.4
  182.5 2.6 add_convert_fusion.5
  185.1 33.8 %experts.7 = (bf16[512,1024]{1,0:T(8,128)(2,1)}, bf16[512,1024]{1,0:T(8,128)(2,1)}, bf16[512,1024]{1,0:T(8,128)(2,1)}, bf16[512,1024]{1,0:T(8,128)(2,1)}, f32[8,...) custom-call(s32[1]{0:T(128)} %bitcast.ep_ref, ...), custom_call_target="tpu_custom_call" | custom-call | flops 28000000000 | bytes 40000000 | tf_op jit(solution)/shard_map/experts/pallas_call | solution.py:253
  221.9 3.7 %all-to-all-start = ((f32[8,8,512]{2,1,0:T(8,128)}), f32[8,8,512]{2,1,0:T(8,128)S(1)}, u32[]{:S(2)}, u32[]{:S(2)}) async-start(f32[8,8,512]{2,1,0:T(8,128)} %gather_fusion.1), calls=%async_computation | async-start | bytes 262144 | tf_op jit(solution)/shard_map/all_to_all | solution.py:511
  226.2 4.5 %all-to-all-done = f32[8,8,512]{2,1,0:T(8,128)S(1)} async-done(((f32[8,8,512]{2,1,0:T(8,128)}), f32[8,8,512]{2,1,0:T(8,128)S(1)}, u32[]{:S(2)}, u32[]{:S(2)}) %all-to-all-start) | async-done | bytes 131104 | tf_op jit(solution)/shard_map/all_to_all | solution.py:511
  232.2 2.6 add_convert_fusion.3
  239.6 2.2 all-to-all-start.1
  241.8 2.6 collective-permute-start.27
  244.7 16.3 %collective-permute-done.24 = bf16[512,1024]{1,0:T(8,128)(2,1)S(1)} collective-permute-done((bf16[512,1024]{1,0:T(8,128)(2,1)}, bf16[512,1024]{1,0:T(8,128)(2,1)S(1)}, u32[]{:S(2)}, u32[]{:S(2)}) %collective-permute-start.24) | collective-permute-done | bytes 1048608 | tf_op jit(solution)/shard_map/ppermute | solution.py:446
  262.1 37.3 %weight_grads.1 = (bf16[8,1024,512]{2,1,0:T(8,128)(2,1)}, bf16[8,256,1024]{2,1,0:T(8,128)(2,1)}) custom-call(s32[8]{0:T(128)} %get-tuple-element.121.refs_0_, s32[8]{0:T(128)} %get-tuple-element.122.refs_1_, s32[8]{0:T(128)} %get-tuple-element.123.refs_2_, s32[8]{0:T(128)} %get-tuple-element.124.refs_3_, ...), custom_call_target="tpu_custom_call" | custom-call | flops 25999998976 | bytes 60000000 | tf_op jit(solution)/shard_map/weight_grads/pallas_call | solution.py:346
  299.4 1.8 fusion.4
  301.2 33.0 %all-to-all-done.1.refs_8_ = f32[8,32,512]{2,1,0:T(8,128)S(1)} async-done(((f32[8,32,512]{2,1,0:T(8,128)}), f32[8,32,512]{2,1,0:T(8,128)S(1)}, u32[]{:S(2)}, u32[]{:S(2)}) %all-to-all-start.1) | async-done | bytes 524320 | tf_op jit(solution)/shard_map/all_to_all | solution.py:515
  334.9 5.6 %router_grad.1 = f32[1024,32]{1,0:T(8,128)S(1)} custom-call(s32[1]{0:T(128)} %bitcast.18.me_ref, bf16[512,1024]{1,0:T(8,128)(2,1)} %refs_0_.1, bf16[512,1024]{1,0:T(8,128)(2,1)} %collective-permute-done.4.xb_hbm.refs_1_, bf16[512,1024]{1,0:T(8,128)(2,1)} %collective-permute-done.xa_hbm.refs_2_, bf16[512,1024]{1,0:T(8,128)(2,1)} %collective-permute-done.3.xb_hbm.refs_3_, ...), custom_call_target="tpu_custom_call" | custom-call | tf_op jit(solution)/shard_map/router_grad/pallas_call | solution.py:420
  341.3 4.8 %add_convert_fusion.1 = bf16[512,1024]{1,0:T(8,128)(2,1)} fusion(bf16[512,1024]{1,0:T(8,128)(2,1)} %copy-done.12, bf16[512,1024]{1,0:T(8,128)(2,1)} %collective-permute-done.23, bf16[512,1024]{1,0:T(8,128)(2,1)} %collective-permute-done.22, bf16[512,1024]{1,0:T(8,128)(2,1)} %collective-permute-done.20, bf16[512,1024]{1,0:T(8,128)(2,1)} %get-tuple-element.146), kind=kLoop, calls=%fused_computation.3 | loop fusion | flops 5242880 | bytes 6291456 | tf_op jit(solution)/shard_map/convert_element_type | solution.py:530
  346.1 4.4 %add_convert_fusion = bf16[512,1024]{1,0:T(8,128)(2,1)} fusion(f32[512,1024]{1,0:T(8,128)S(1)} %copy-done.7, bf16[512,1024]{1,0:T(8,128)(2,1)} %collective-permute-done.25, bf16[512,1024]{1,0:T(8,128)(2,1)} %collective-permute-done.27, bf16[512,1024]{1,0:T(8,128)(2,1)} %collective-permute-done.26, bf16[512,1024]{1,0:T(8,128)(2,1)} %collective-permute-done.21, ...), kind=kLoop, calls=%fused_computation.2 | loop fusion | flops 5767168 | bytes 8388608 | tf_op jit(solution)/shard_map/convert_element_type | solution.py:530
  (141 shorter events, 30.8 us)
Async XLA Ops:
  6.8 54.3 %collective-permute-start.1 = (bf16[576,1024]{1,0:T(8,128)(2,1)S(1)}, bf16[576,1024]{1,0:T(8,128)(2,1)}, u32[]{:S(2)}, u32[]{:S(2)}) collective-permute-start(bf16[576,1024]{1,0:T(8,128)(2,1)S(1)} %get-tuple-element.89.da_hbm), channel_id=1, source_target_pairs={{0,5},{1,4},{2,7},{3,6},{4,1},{5,0},{6,3},{7,2}} | collective-permute-start | bytes 3538952 | tf_op jit(solution)/shard_map/ppermute | solution.py:446
  9.6 53.1 %collective-permute-start.5 = (bf16[576,1024]{1,0:T(8,128)(2,1)S(1)}, bf16[576,1024]{1,0:T(8,128)(2,1)S(1)}, u32[]{:S(2)}, u32[]{:S(2)}) collective-permute-start(bf16[576,1024]{1,0:T(8,128)(2,1)S(1)} %get-tuple-element.89.da_hbm), channel_id=1, source_target_pairs={{0,1},{1,0},{2,3},{3,2},{4,5},{5,4},{6,7},{7,6}} | collective-permute-start | bytes 3538952 | tf_op jit(solution)/shard_map/ppermute | solution.py:446
  10.3 48.4 %collective-permute-start = (bf16[512,1024]{1,0:T(8,128)(2,1)}, bf16[512,1024]{1,0:T(8,128)(2,1)}, u32[]{:S(2)}, u32[]{:S(2)}) collective-permute-start(bf16[512,1024]{1,0:T(8,128)(2,1)} %refs_0_.1), channel_id=1, source_target_pairs={{0,4},{1,5},{2,6},{3,7},{4,0},{5,1},{6,2},{7,3}} | collective-permute-start | bytes 3145736 | tf_op jit(solution)/shard_map/ppermute | solution.py:446
  11.2 47.6 %collective-permute-start.8 = (bf16[512,1024]{1,0:T(8,128)(2,1)}, bf16[512,1024]{1,0:T(8,128)(2,1)}, u32[]{:S(2)}, u32[]{:S(2)}) collective-permute-start(bf16[512,1024]{1,0:T(8,128)(2,1)} %refs_0_.1), channel_id=1, source_target_pairs={{0,2},{1,3},{2,0},{3,1},{4,6},{5,7},{6,4},{7,5}} | collective-permute-start | bytes 3145736 | tf_op jit(solution)/shard_map/ppermute | solution.py:446
  12.6 48.6 %collective-permute-start.4 = (bf16[512,1024]{1,0:T(8,128)(2,1)}, bf16[512,1024]{1,0:T(8,128)(2,1)}, u32[]{:S(2)}, u32[]{:S(2)}) collective-permute-start(bf16[512,1024]{1,0:T(8,128)(2,1)} %refs_0_.1), channel_id=1, source_target_pairs={{0,1},{1,0},{2,3},{3,2},{4,5},{5,4},{6,7},{7,6}} | collective-permute-start | bytes 3145736 | tf_op jit(solution)/shard_map/ppermute | solution.py:446
  58.7 42.4 %collective-permute-start.3 = (bf16[512,1024]{1,0:T(8,128)(2,1)}, bf16[512,1024]{1,0:T(8,128)(2,1)}, u32[]{:S(2)}, u32[]{:S(2)}) collective-permute-start(bf16[512,1024]{1,0:T(8,128)(2,1)} %collective-permute-done.xa_hbm.refs_2_), channel_id=1, source_target_pairs={{0,1},{1,0},{2,3},{3,2},{4,5},{5,4},{6,7},{7,6}} | collective-permute-start | bytes 3145736 | tf_op jit(solution)/shard_map/ppermute | solution.py:446
  58.7 75.0 %collective-permute-start.9 = (bf16[512,1024]{1,0:T(8,128)(2,1)}, bf16[512,1024]{1,0:T(8,128)(2,1)}, u32[]{:S(2)}, u32[]{:S(2)}) collective-permute-start(bf16[512,1024]{1,0:T(8,128)(2,1)} %collective-permute-done.8.xa_hbm.refs_6_), channel_id=1, source_target_pairs={{0,4},{1,5},{2,6},{3,7},{4,0},{5,1},{6,2},{7,3}} | collective-permute-start | bytes 3145736 | tf_op jit(solution)/shard_map/ppermute | solution.py:446
  61.1 40.0 %collective-permute-start.2 = (bf16[576,1024]{1,0:T(8,128)(2,1)}, bf16[576,1024]{1,0:T(8,128)(2,1)}, u32[]{:S(2)}, u32[]{:S(2)}) collective-permute-start(bf16[576,1024]{1,0:T(8,128)(2,1)} %collective-permute-done.1.db_hbm), channel_id=1, source_target_pairs={{0,1},{1,0},{2,3},{3,2},{4,5},{5,4},{6,7},{7,6}} | collective-permute-start | bytes 3538952 | tf_op jit(solution)/shard_map/ppermute | solution.py:446
  61.3 72.3 %collective-permute-start.10 = (bf16[576,1024]{1,0:T(8,128)(2,1)}, bf16[576,1024]{1,0:T(8,128)(2,1)}, u32[]{:S(2)}, u32[]{:S(2)}) collective-permute-start(bf16[576,1024]{1,0:T(8,128)(2,1)} %collective-permute-done.1.db_hbm), channel_id=1, source_target_pairs={{0,2},{1,3},{2,0},{3,1},{4,6},{5,7},{6,4},{7,5}} | collective-permute-start | bytes 3538952 | tf_op jit(solution)/shard_map/ppermute | solution.py:446
  133.6 8.4 %collective-permute-start.11 = (bf16[576,1024]{1,0:T(8,128)(2,1)}, bf16[576,1024]{1,0:T(8,128)(2,1)}, u32[]{:S(2)}, u32[]{:S(2)}) collective-permute-start(bf16[576,1024]{1,0:T(8,128)(2,1)} %collective-permute-done.10.db_hbm), channel_id=1, source_target_pairs={{0,1},{1,0},{2,3},{3,2},{4,5},{5,4},{6,7},{7,6}} | collective-permute-start | bytes 3538952 | tf_op jit(solution)/shard_map/ppermute | solution.py:446
  133.7 8.3 %collective-permute-start.12 = (bf16[512,1024]{1,0:T(8,128)(2,1)}, bf16[512,1024]{1,0:T(8,128)(2,1)}, u32[]{:S(2)}, u32[]{:S(2)}) collective-permute-start(bf16[512,1024]{1,0:T(8,128)(2,1)} %collective-permute-done.9.xa_hbm.refs_4_), channel_id=1, source_target_pairs={{0,1},{1,0},{2,3},{3,2},{4,5},{5,4},{6,7},{7,6}} | collective-permute-start | bytes 3145736 | tf_op jit(solution)/shard_map/ppermute | solution.py:446
  134.1 43.4 %collective-permute-start.15 = (bf16[576,1024]{1,0:T(8,128)(2,1)}, bf16[576,1024]{1,0:T(8,128)(2,1)}, u32[]{:S(2)}, u32[]{:S(2)}) collective-permute-start(bf16[576,1024]{1,0:T(8,128)(2,1)} %copy-done.5), channel_id=1, source_target_pairs={{0,3},{1,2},{2,1},{3,0},{4,7},{5,6},{6,5},{7,4}} | collective-permute-start | bytes 3538952 | tf_op jit(solution)/shard_map/ppermute | solution.py:446
  218.9 11.8 %collective-permute-start.19 = (bf16[512,1024]{1,0:T(8,128)(2,1)}, bf16[512,1024]{1,0:T(8,128)(2,1)S(1)}, u32[]{:S(2)}, u32[]{:S(2)}) collective-permute-start(bf16[512,1024]{1,0:T(8,128)(2,1)} %get-tuple-element.110), channel_id=1, source_target_pairs={{0,1},{1,0},{2,3},{3,2},{4,5},{5,4},{6,7},{7,6}} | collective-permute-start | bytes 3145736 | tf_op jit(solution)/shard_map/ppermute | solution.py:446
  219.0 13.1 %collective-permute-start.18 = (bf16[512,1024]{1,0:T(8,128)(2,1)}, bf16[512,1024]{1,0:T(8,128)(2,1)}, u32[]{:S(2)}, u32[]{:S(2)}) collective-permute-start(bf16[512,1024]{1,0:T(8,128)(2,1)} %get-tuple-element.108), channel_id=1, source_target_pairs={{0,1},{1,0},{2,3},{3,2},{4,5},{5,4},{6,7},{7,6}} | collective-permute-start | bytes 3145736 | tf_op jit(solution)/shard_map/ppermute | solution.py:446
  221.9 8.7 %all-to-all-start = ((f32[8,8,512]{2,1,0:T(8,128)}), f32[8,8,512]{2,1,0:T(8,128)S(1)}, u32[]{:S(2)}, u32[]{:S(2)}) async-start(f32[8,8,512]{2,1,0:T(8,128)} %gather_fusion.1), calls=%async_computation | async-start | bytes 262144 | tf_op jit(solution)/shard_map/all_to_all | solution.py:511
  225.7 16.1 %collective-permute-start.20 = (bf16[512,1024]{1,0:T(8,128)(2,1)}, bf16[512,1024]{1,0:T(8,128)(2,1)}, u32[]{:S(2)}, u32[]{:S(2)}) collective-permute-start(bf16[512,1024]{1,0:T(8,128)(2,1)} %get-tuple-element.143), channel_id=1, source_target_pairs={{0,1},{1,0},{2,3},{3,2},{4,5},{5,4},{6,7},{7,6}} | collective-permute-start | bytes 3145736 | tf_op jit(solution)/shard_map/ppermute | solution.py:446
  226.2 18.2 %collective-permute-start.21 = (bf16[512,1024]{1,0:T(8,128)(2,1)}, bf16[512,1024]{1,0:T(8,128)(2,1)}, u32[]{:S(2)}, u32[]{:S(2)}) collective-permute-start(bf16[512,1024]{1,0:T(8,128)(2,1)} %get-tuple-element.145), channel_id=1, source_target_pairs={{0,1},{1,0},{2,3},{3,2},{4,5},{5,4},{6,7},{7,6}} | collective-permute-start | bytes 3145736 | tf_op jit(solution)/shard_map/ppermute | solution.py:446
  234.8 26.2 %collective-permute-start.24 = (bf16[512,1024]{1,0:T(8,128)(2,1)}, bf16[512,1024]{1,0:T(8,128)(2,1)S(1)}, u32[]{:S(2)}, u32[]{:S(2)}) collective-permute-start(bf16[512,1024]{1,0:T(8,128)(2,1)} %add_convert_fusion.3), channel_id=1, source_target_pairs={{0,2},{1,3},{2,0},{3,1},{4,6},{5,7},{6,4},{7,5}} | collective-permute-start | bytes 3145736 | tf_op jit(solution)/shard_map/ppermute | solution.py:446
  235.6 110.5 %collective-permute-start.26 = (bf16[512,1024]{1,0:T(8,128)(2,1)}, bf16[512,1024]{1,0:T(8,128)(2,1)}, u32[]{:S(2)}, u32[]{:S(2)}) collective-permute-start(bf16[512,1024]{1,0:T(8,128)(2,1)} %add_convert_fusion.6), channel_id=1, source_target_pairs={{0,5},{1,4},{2,7},{3,6},{4,1},{5,0},{6,3},{7,2}} | collective-permute-start | bytes 3145736 | tf_op jit(solution)/shard_map/ppermute | solution.py:446
  235.6 105.7 %collective-permute-start.22 = (bf16[512,1024]{1,0:T(8,128)(2,1)}, bf16[512,1024]{1,0:T(8,128)(2,1)}, u32[]{:S(2)}, u32[]{:S(2)}) collective-permute-start(bf16[512,1024]{1,0:T(8,128)(2,1)} %add_convert_fusion.7), channel_id=1, source_target_pairs={{0,4},{1,5},{2,6},{3,7},{4,0},{5,1},{6,2},{7,3}} | collective-permute-start | bytes 3145736 | tf_op jit(solution)/shard_map/ppermute | solution.py:446
  239.6 94.6 %all-to-all-start.1 = ((f32[8,32,512]{2,1,0:T(8,128)}), f32[8,32,512]{2,1,0:T(8,128)S(1)}, u32[]{:S(2)}, u32[]{:S(2)}) async-start(f32[8,32,512]{2,1,0:T(8,128)} %broadcast_in_dim.26), calls=%async_computation.1 | async-start | bytes 1048576 | tf_op jit(solution)/shard_map/all_to_all | solution.py:515
  241.8 104.3 %collective-permute-start.27 = (bf16[512,1024]{1,0:T(8,128)(2,1)}, bf16[512,1024]{1,0:T(8,128)(2,1)}, u32[]{:S(2)}, u32[]{:S(2)}) collective-permute-start(bf16[512,1024]{1,0:T(8,128)(2,1)} %add_convert_fusion.4), channel_id=1, source_target_pairs={{0,7},{1,6},{2,5},{3,4},{4,3},{5,2},{6,1},{7,0}} | collective-permute-start | bytes 3145736 | tf_op jit(solution)/shard_map/ppermute | solution.py:446
  244.4 96.9 %collective-permute-start.23 = (bf16[512,1024]{1,0:T(8,128)(2,1)}, bf16[512,1024]{1,0:T(8,128)(2,1)}, u32[]{:S(2)}, u32[]{:S(2)}) collective-permute-start(bf16[512,1024]{1,0:T(8,128)(2,1)} %add_convert_fusion.5), channel_id=1, source_target_pairs={{0,6},{1,7},{2,4},{3,5},{4,2},{5,3},{6,0},{7,1}} | collective-permute-start | bytes 3145736 | tf_op jit(solution)/shard_map/ppermute | solution.py:446
  261.1 79.4 %collective-permute-start.25 = (bf16[512,1024]{1,0:T(8,128)(2,1)}, bf16[512,1024]{1,0:T(8,128)(2,1)}, u32[]{:S(2)}, u32[]{:S(2)}) collective-permute-start(bf16[512,1024]{1,0:T(8,128)(2,1)} %add_convert_fusion.2), channel_id=1, source_target_pairs={{0,3},{1,2},{2,1},{3,0},{4,7},{5,6},{6,5},{7,4}} | collective-permute-start | bytes 3145736 | tf_op jit(solution)/shard_map/ppermute | solution.py:446
  (34 other events, 331.6 us)

commit v3 on v2

--- a/solution.py
+++ b/solution.py
@@ -146,7 +146,7 @@
         gate_on = jnp.where(gate < LIMIT, 1.0, jnp.where(gate == LIMIT, 0.5, 0.0))
         up_abs = jnp.abs(up)
         up_on = jnp.where(up_abs < LIMIT, 1.0, jnp.where(up_abs == LIMIT, 0.5, 0.0))
-        d_gate = d_act * u1 * (sg * (1.0 + ALPHA * g * (1.0 - sg))) * gate_on
+        d_gate = d_act * u1 * (sg + ALPHA * gs * (1.0 - sg)) * gate_on
         d_up = d_act * gs * up_on
         gb1_ref[0, :, :half] += jnp.sum(d_gate, axis=0, keepdims=True)
         gb1_ref[0, :, half:] += jnp.sum(d_up, axis=0, keepdims=True)
@@ -509,23 +509,25 @@
         slot_of = jnp.array([rel.index(m) for m in range(n_dev)], jnp.int32)
         dg_abs = dg_rel[slot_of[jnp.arange(n_dev) ^ me]]
         dg_back = lax.all_to_all(dg_abs, ('ep', 'tp'), 0, 0, tiled=True)
+        sum_3, dg_back = lax.optimization_barrier((both(3), dg_back))
         d_gate = jnp.sum(dg_back.reshape(ep_count, tp_count, n_e, toks), axis=1).reshape(n_experts, toks)
         d_logits = w_full * (d_gate - jnp.sum(w_full * d_gate, axis=0, keepdims=True))
-        sum_3, d_logits, last = lax.optimization_barrier((both(3), d_logits, saved[3]))
+        sum_3, d_logits, last = lax.optimization_barrier((sum_3, d_logits, saved[3]))
         d_all = lax.all_to_all(jnp.broadcast_to(d_logits[None], (n_dev, *d_logits.shape)), ('ep', 'tp'), 0, 0, tiled=True)
         got_3 = hop(3, *sum_3)
         gw1, gw2 = run_wgrad(nts, [*saved[:3], last], split_mat.T)
+        gw1, gb1s, gb2s, d_late, own, got_1, got_2 = lax.optimization_barrier((gw1, gb1s, gb2s, d_logits, part[0], got_1, got_2))
         gb1 = functools.reduce(jnp.add, gb1s)[:, 0, :]
         gb1 = jnp.stack([gb1[:, :half], gb1[:, half:]], axis=2).reshape(n_e, wide)
         gb2 = functools.reduce(jnp.add, gb2s)
 
         wide_sum = lambda *terms: functools.reduce(jnp.add, [t.astype(F32) for t in terms])
-        via_router = jnp.einsum('et,de->td', d_logits.astype(BF), w_router, preferred_element_type=F32)
-        d_all, gw1, own = lax.optimization_barrier((d_all, gw1, part[0]))
+        via_router = jnp.einsum('et,de->td', d_late.astype(BF), w_router, preferred_element_type=F32)
+        dx_most = wide_sum(own[2], own[3], got_1[1], got_2[1], via_router)
         gwr = run_router_grad(me.astype(jnp.int32)[None], rel, [p[k] for p in pairs for k in (0, 2)], d_all)
-        gwr, got_3 = lax.optimization_barrier((gwr, got_3))
+        gwr, dx_most, got_3 = lax.optimization_barrier((gwr, dx_most, got_3))
         moe = wide_sum(own[0], own[1], got_1[0], got_2[0], got_3[0])
-        d_x = wide_sum(own[2], own[3], got_1[1], got_2[1], got_3[1], via_router)
+        d_x = dx_most + got_3[1].astype(F32)
         gbr = jnp.sum(d_all, axis=(0, 2))
         return (moe.astype(BF), d_x.astype(BF), gw1, gb1, gw2, gb2, gwr, gbr)
 

time: 351 us -> 382 us (1.088)
  waiting for transfers between devices: 97.9 us -> 125 us
  starting transfers between devices: 28 us -> 35 us
    all_to_all x1, waiting for transfers between devices: 4.46 us -> 33.4 us  [device_fn(): dg_back = lax.all_to_all(dg_abs, ('ep', 'tp'), 0, 0, tiled=True)]
    ppermute x28, waiting for transfers between devices: 60.5 us -> 47.4 us  [flip(): lax.ppermute(arr, ('tp', 'ep'), [(s, s ^ turned) for s in range(n_dev)])]
    all_to_all x1, waiting for transfers between devices: 33 us -> 44.3 us  [device_fn(): lax.all_to_all(jnp.broadcast_to(d_logits[None], (n_dev, *d_logits.shape))...]
    ppermute x28, starting transfers between devices: 22.1 us -> 27.9 us  [flip(): lax.ppermute(arr, ('tp', 'ep'), [(s, s ^ turned) for s in range(n_dev)])]
    convert_element_type x2 -> x1, other arithmetic: 9.17 us -> 5.68 us  [device_fn(): return (moe.astype(BF), d_x.astype(BF), gw1, gb1, gw2, gb2, gwr, gbr)]
  transfers between devices with their start and end apart: 30 -> 30, of which waited for: 5 -> 6; matrix products, arithmetic and copies ran while one was open for 9% -> 7% of each run, Pallas kernels for 42% -> 39%
where the time goes in v3:
time: 382 us; the launch traced here: 381 us
  Pallas kernels  182 us (48%)
  waiting for transfers between devices  125 us (33%)
  starting transfers between devices  35 us (9%)
  other arithmetic  22.7 us (6%)
  local copies, waits for them, and re-layouts  12.3 us (3%)
    pallas_call x4, Pallas kernels, run_chunk(): pl.pallas_call(functools.partial(chunk_kernel, first, toks), grid_spec=pl...  138 us
    ppermute x28, waiting for transfers between devices, flip(): lax.ppermute(arr, ('tp', 'ep'), [(s, s ^ turned) for s in range(n_dev)])  47.4 us
    all_to_all x1, waiting for transfers between devices, device_fn(): lax.all_to_all(jnp.broadcast_to(d_logits[None], (n_dev, *d_logits.shape))...  44.3 us
    pallas_call x1, Pallas kernels, run_wgrad(): pl.pallas_call(functools.partial(wgrad_kernel, n_c), grid_spec=pltpu.Pref...  37.4 us
    all_to_all x1, waiting for transfers between devices, device_fn(): dg_back = lax.all_to_all(dg_abs, ('ep', 'tp'), 0, 0, tiled=True)  33.4 us
    ppermute x28, starting transfers between devices, flip(): lax.ppermute(arr, ('tp', 'ep'), [(s, s ^ turned) for s in range(n_dev)])  27.9 us
    convert_element_type x6, other arithmetic, both(): add = lambda a, b: (a.astype(F32) + b.astype(F32)).astype(BF)  13.9 us
  transfers between devices with their start and end apart: 30, of which 6 were waited for; matrix products, arithmetic and copies ran while one was open for 7% of the time, Pallas kernels for 39%

profile of v3, /device:TPU:0, one launch (start us, length us, event | category | flops | bytes accessed | tf_op | source)
XLA Modules:
  0.0 381.4 jit_solution(3756066793651242480)
XLA Ops:
  4.9 1.9 pack.1
  6.8 2.8 collective-permute-start.3
  15.7 43.0 %collective-permute-done.2.xa_hbm.refs_2_ = bf16[512,1024]{1,0:T(8,128)(2,1)} collective-permute-done((bf16[512,1024]{1,0:T(8,128)(2,1)}, bf16[512,1024]{1,0:T(8,128)(2,1)}, u32[]{:S(2)}, u32[]{:S(2)}) %collective-permute-start.2) | collective-permute-done | bytes 1048608 | tf_op jit(solution)/shard_map/ppermute | solution.py:446
  58.7 2.4 collective-permute-start.9
  63.8 37.3 %experts.4 = (bf16[512,1024]{1,0:T(8,128)(2,1)}, bf16[512,1024]{1,0:T(8,128)(2,1)}, bf16[512,1024]{1,0:T(8,128)(2,1)}, bf16[512,1024]{1,0:T(8,128)(2,1)}, f32[8,...) custom-call(s32[1]{0:T(128)} %bitcast.ep_ref, ...), custom_call_target="tpu_custom_call" | custom-call | flops 28000000000 | bytes 40000000 | tf_op jit(solution)/shard_map/experts/pallas_call | solution.py:253
  101.1 31.8 %experts.5 = (bf16[512,1024]{1,0:T(8,128)(2,1)}, bf16[512,1024]{1,0:T(8,128)(2,1)}, bf16[512,1024]{1,0:T(8,128)(2,1)}, bf16[512,1024]{1,0:T(8,128)(2,1)}, f32[8,...) custom-call(s32[1]{0:T(128)} %bitcast.ep_ref, ...), custom_call_target="tpu_custom_call" | custom-call | flops 28000000000 | bytes 40000000 | tf_op jit(solution)/shard_map/experts/pallas_call | solution.py:253
  134.0 3.9 %collective-permute-start.15 = (bf16[576,1024]{1,0:T(8,128)(2,1)}, bf16[576,1024]{1,0:T(8,128)(2,1)}, u32[]{:S(2)}, u32[]{:S(2)}) collective-permute-start(bf16[576,1024]{1,0:T(8,128)(2,1)} %copy-done.5), channel_id=1, source_target_pairs={{0,3},{1,2},{2,1},{3,0},{4,7},{5,6},{6,5},{7,4}} | collective-permute-start | bytes 3538952 | tf_op jit(solution)/shard_map/ppermute | solution.py:446
  137.9 2.6 add_convert_fusion.6
  141.9 34.8 %experts.6 = (bf16[512,1024]{1,0:T(8,128)(2,1)}, bf16[512,1024]{1,0:T(8,128)(2,1)}, bf16[512,1024]{1,0:T(8,128)(2,1)}, bf16[512,1024]{1,0:T(8,128)(2,1)}, f32[8,...) custom-call(s32[1]{0:T(128)} %bitcast.ep_ref, ...), custom_call_target="tpu_custom_call" | custom-call | flops 28000000000 | bytes 40000000 | tf_op jit(solution)/shard_map/experts/pallas_call | solution.py:253
  179.8 2.9 add_convert_fusion.4
  184.5 33.7 %experts.7 = (bf16[512,1024]{1,0:T(8,128)(2,1)}, bf16[512,1024]{1,0:T(8,128)(2,1)}, bf16[512,1024]{1,0:T(8,128)(2,1)}, bf16[512,1024]{1,0:T(8,128)(2,1)}, f32[8,...) custom-call(s32[1]{0:T(128)} %bitcast.ep_ref, ...), custom_call_target="tpu_custom_call" | custom-call | flops 28000000000 | bytes 40000000 | tf_op jit(solution)/shard_map/experts/pallas_call | solution.py:253
  222.1 4.9 %all-to-all-start = ((f32[8,8,512]{2,1,0:T(8,128)}), f32[8,8,512]{2,1,0:T(8,128)S(1)}, u32[]{:S(2)}, u32[]{:S(2)}) async-start(f32[8,8,512]{2,1,0:T(8,128)} %gather_fusion.1), calls=%async_computation | async-start | bytes 262144 | tf_op jit(solution)/shard_map/all_to_all | solution.py:511
  228.8 2.9 add_convert_fusion.2
  233.1 2.6 add_convert_fusion.3
  235.8 33.4 %all-to-all-done = f32[8,8,512]{2,1,0:T(8,128)S(1)} async-done(((f32[8,8,512]{2,1,0:T(8,128)}), f32[8,8,512]{2,1,0:T(8,128)S(1)}, u32[]{:S(2)}, u32[]{:S(2)}) %all-to-all-start) | async-done | bytes 131104 | tf_op jit(solution)/shard_map/all_to_all | solution.py:511
  269.2 3.4 collective-permute-start.25
  272.6 37.4 %weight_grads.1 = (bf16[8,1024,512]{2,1,0:T(8,128)(2,1)}, bf16[8,256,1024]{2,1,0:T(8,128)(2,1)}) custom-call(s32[8]{0:T(128)} %get-tuple-element.106.refs_0_, s32[8]{0:T(128)} %get-tuple-element.108.refs_1_, s32[8]{0:T(128)} %get-tuple-element.117.refs_2_, s32[8]{0:T(128)} %get-tuple-element.126.refs_3_, ...), custom_call_target="tpu_custom_call" | custom-call | flops 25999998976 | bytes 60000000 | tf_op jit(solution)/shard_map/weight_grads/pallas_call | solution.py:346
  310.0 2.6 collective-permute-done.23
  312.7 3.8 collective-permute-start.26
  317.8 2.2 all-to-all-start.1
  321.6 2.8 add_add_fusion
  324.4 44.3 %all-to-all-done.1.refs_8_ = f32[8,32,512]{2,1,0:T(8,128)S(1)} async-done(((f32[8,32,512]{2,1,0:T(8,128)}), f32[8,32,512]{2,1,0:T(8,128)S(1)}, u32[]{:S(2)}, u32[]{:S(2)}) %all-to-all-start.1) | async-done | bytes 524320 | tf_op jit(solution)/shard_map/all_to_all | solution.py:516
  368.7 5.6 %router_grad.1 = f32[1024,32]{1,0:T(8,128)S(1)} custom-call(s32[1]{0:T(128)} %bitcast.18.me_ref, bf16[512,1024]{1,0:T(8,128)(2,1)} %refs_0_.1, bf16[512,1024]{1,0:T(8,128)(2,1)} %collective-permute-done.xb_hbm.refs_1_, bf16[512,1024]{1,0:T(8,128)(2,1)} %collective-permute-done.2.xa_hbm.refs_2_, bf16[512,1024]{1,0:T(8,128)(2,1)} %collective-permute-done.5.xb_hbm.refs_3_, ...), custom_call_target="tpu_custom_call" | custom-call | tf_op jit(solution)/shard_map/router_grad/pallas_call | solution.py:420
  375.8 5.7 %add_convert_fusion = (bf16[512,1024]{1,0:T(8,128)(2,1)}, bf16[512,1024]{1,0:T(8,128)(2,1)}) fusion(f32[512,1024]{1,0:T(8,128)S(1)} %add_add_fusion, bf16[512,1024]{1,0:T(8,128)(2,1)} %collective-permute-done.27, bf16[512,1024]{1,0:T(8,128)(2,1)} %collective-permute-done.26, bf16[512,1024]{1,0:T(8,128)(2,1)} %collective-permute-done.24, ...), kind=kLoop, calls=%fused_computation.2 | loop fusion | flops 6815744 | bytes 10485760 | tf_op jit(solution)/shard_map/convert_element_type | solution.py:532
  (134 shorter events, 31.7 us)
Async XLA Ops:
  6.8 54.3 %collective-permute-start.3 = (bf16[576,1024]{1,0:T(8,128)(2,1)S(1)}, bf16[576,1024]{1,0:T(8,128)(2,1)}, u32[]{:S(2)}, u32[]{:S(2)}) collective-permute-start(bf16[576,1024]{1,0:T(8,128)(2,1)S(1)} %get-tuple-element.105.da_hbm), channel_id=1, source_target_pairs={{0,5},{1,4},{2,7},{3,6},{4,1},{5,0},{6,3},{7,2}} | collective-permute-start | bytes 3538952 | tf_op jit(solution)/shard_map/ppermute | solution.py:446
  9.6 53.1 %collective-permute-start.1 = (bf16[576,1024]{1,0:T(8,128)(2,1)S(1)}, bf16[576,1024]{1,0:T(8,128)(2,1)S(1)}, u32[]{:S(2)}, u32[]{:S(2)}) collective-permute-start(bf16[576,1024]{1,0:T(8,128)(2,1)S(1)} %get-tuple-element.105.da_hbm), channel_id=1, source_target_pairs={{0,1},{1,0},{2,3},{3,2},{4,5},{5,4},{6,7},{7,6}} | collective-permute-start | bytes 3538952 | tf_op jit(solution)/shard_map/ppermute | solution.py:446
  10.3 48.4 %collective-permute-start.2 = (bf16[512,1024]{1,0:T(8,128)(2,1)}, bf16[512,1024]{1,0:T(8,128)(2,1)}, u32[]{:S(2)}, u32[]{:S(2)}) collective-permute-start(bf16[512,1024]{1,0:T(8,128)(2,1)} %refs_0_.1), channel_id=1, source_target_pairs={{0,4},{1,5},{2,6},{3,7},{4,0},{5,1},{6,2},{7,3}} | collective-permute-start | bytes 3145736 | tf_op jit(solution)/shard_map/ppermute | solution.py:446
  11.2 47.6 %collective-permute-start.8 = (bf16[512,1024]{1,0:T(8,128)(2,1)}, bf16[512,1024]{1,0:T(8,128)(2,1)}, u32[]{:S(2)}, u32[]{:S(2)}) collective-permute-start(bf16[512,1024]{1,0:T(8,128)(2,1)} %refs_0_.1), channel_id=1, source_target_pairs={{0,2},{1,3},{2,0},{3,1},{4,6},{5,7},{6,4},{7,5}} | collective-permute-start | bytes 3145736 | tf_op jit(solution)/shard_map/ppermute | solution.py:446
  12.6 48.6 %collective-permute-start = (bf16[512,1024]{1,0:T(8,128)(2,1)}, bf16[512,1024]{1,0:T(8,128)(2,1)}, u32[]{:S(2)}, u32[]{:S(2)}) collective-permute-start(bf16[512,1024]{1,0:T(8,128)(2,1)} %refs_0_.1), channel_id=1, source_target_pairs={{0,1},{1,0},{2,3},{3,2},{4,5},{5,4},{6,7},{7,6}} | collective-permute-start | bytes 3145736 | tf_op jit(solution)/shard_map/ppermute | solution.py:446
  58.7 42.4 %collective-permute-start.5 = (bf16[512,1024]{1,0:T(8,128)(2,1)}, bf16[512,1024]{1,0:T(8,128)(2,1)}, u32[]{:S(2)}, u32[]{:S(2)}) collective-permute-start(bf16[512,1024]{1,0:T(8,128)(2,1)} %collective-permute-done.2.xa_hbm.refs_2_), channel_id=1, source_target_pairs={{0,1},{1,0},{2,3},{3,2},{4,5},{5,4},{6,7},{7,6}} | collective-permute-start | bytes 3145736 | tf_op jit(solution)/shard_map/ppermute | solution.py:446
  58.7 74.8 %collective-permute-start.9 = (bf16[512,1024]{1,0:T(8,128)(2,1)}, bf16[512,1024]{1,0:T(8,128)(2,1)}, u32[]{:S(2)}, u32[]{:S(2)}) collective-permute-start(bf16[512,1024]{1,0:T(8,128)(2,1)} %collective-permute-done.8.xa_hbm.refs_6_), channel_id=1, source_target_pairs={{0,4},{1,5},{2,6},{3,7},{4,0},{5,1},{6,2},{7,3}} | collective-permute-start | bytes 3145736 | tf_op jit(solution)/shard_map/ppermute | solution.py:446
  61.1 40.0 %collective-permute-start.4 = (bf16[576,1024]{1,0:T(8,128)(2,1)}, bf16[576,1024]{1,0:T(8,128)(2,1)}, u32[]{:S(2)}, u32[]{:S(2)}) collective-permute-start(bf16[576,1024]{1,0:T(8,128)(2,1)} %collective-permute-done.3.db_hbm), channel_id=1, source_target_pairs={{0,1},{1,0},{2,3},{3,2},{4,5},{5,4},{6,7},{7,6}} | collective-permute-start | bytes 3538952 | tf_op jit(solution)/shard_map/ppermute | solution.py:446
  61.3 72.2 %collective-permute-start.10 = (bf16[576,1024]{1,0:T(8,128)(2,1)}, bf16[576,1024]{1,0:T(8,128)(2,1)}, u32[]{:S(2)}, u32[]{:S(2)}) collective-permute-start(bf16[576,1024]{1,0:T(8,128)(2,1)} %collective-permute-done.3.db_hbm), channel_id=1, source_target_pairs={{0,2},{1,3},{2,0},{3,1},{4,6},{5,7},{6,4},{7,5}} | collective-permute-start | bytes 3538952 | tf_op jit(solution)/shard_map/ppermute | solution.py:446
  133.5 8.4 %collective-permute-start.11 = (bf16[576,1024]{1,0:T(8,128)(2,1)}, bf16[576,1024]{1,0:T(8,128)(2,1)}, u32[]{:S(2)}, u32[]{:S(2)}) collective-permute-start(bf16[576,1024]{1,0:T(8,128)(2,1)} %collective-permute-done.10.db_hbm), channel_id=1, source_target_pairs={{0,1},{1,0},{2,3},{3,2},{4,5},{5,4},{6,7},{7,6}} | collective-permute-start | bytes 3538952 | tf_op jit(solution)/shard_map/ppermute | solution.py:446
  133.5 8.4 %collective-permute-start.12 = (bf16[512,1024]{1,0:T(8,128)(2,1)}, bf16[512,1024]{1,0:T(8,128)(2,1)}, u32[]{:S(2)}, u32[]{:S(2)}) collective-permute-start(bf16[512,1024]{1,0:T(8,128)(2,1)} %collective-permute-done.9.xa_hbm.refs_4_), channel_id=1, source_target_pairs={{0,1},{1,0},{2,3},{3,2},{4,5},{5,4},{6,7},{7,6}} | collective-permute-start | bytes 3145736 | tf_op jit(solution)/shard_map/ppermute | solution.py:446
  134.0 43.3 %collective-permute-start.15 = (bf16[576,1024]{1,0:T(8,128)(2,1)}, bf16[576,1024]{1,0:T(8,128)(2,1)}, u32[]{:S(2)}, u32[]{:S(2)}) collective-permute-start(bf16[576,1024]{1,0:T(8,128)(2,1)} %copy-done.5), channel_id=1, source_target_pairs={{0,3},{1,2},{2,1},{3,0},{4,7},{5,6},{6,5},{7,4}} | collective-permute-start | bytes 3538952 | tf_op jit(solution)/shard_map/ppermute | solution.py:446
  218.2 8.8 %collective-permute-start.19 = (bf16[512,1024]{1,0:T(8,128)(2,1)}, bf16[512,1024]{1,0:T(8,128)(2,1)}, u32[]{:S(2)}, u32[]{:S(2)}) collective-permute-start(bf16[512,1024]{1,0:T(8,128)(2,1)} %get-tuple-element.133), channel_id=1, source_target_pairs={{0,1},{1,0},{2,3},{3,2},{4,5},{5,4},{6,7},{7,6}} | collective-permute-start | bytes 3145736 | tf_op jit(solution)/shard_map/ppermute | solution.py:446
  218.2 13.4 %collective-permute-start.18 = (bf16[512,1024]{1,0:T(8,128)(2,1)}, bf16[512,1024]{1,0:T(8,128)(2,1)}, u32[]{:S(2)}, u32[]{:S(2)}) collective-permute-start(bf16[512,1024]{1,0:T(8,128)(2,1)} %get-tuple-element.131), channel_id=1, source_target_pairs={{0,1},{1,0},{2,3},{3,2},{4,5},{5,4},{6,7},{7,6}} | collective-permute-start | bytes 3145736 | tf_op jit(solution)/shard_map/ppermute | solution.py:446
  218.8 50.4 %collective-permute-start.20 = (bf16[512,1024]{1,0:T(8,128)(2,1)}, bf16[512,1024]{1,0:T(8,128)(2,1)}, u32[]{:S(2)}, u32[]{:S(2)}) collective-permute-start(bf16[512,1024]{1,0:T(8,128)(2,1)} %get-tuple-element.170), channel_id=1, source_target_pairs={{0,1},{1,0},{2,3},{3,2},{4,5},{5,4},{6,7},{7,6}} | collective-permute-start | bytes 3145736 | tf_op jit(solution)/shard_map/ppermute | solution.py:446
  218.8 91.2 %collective-permute-start.21 = (bf16[512,1024]{1,0:T(8,128)(2,1)}, bf16[512,1024]{1,0:T(8,128)(2,1)}, u32[]{:S(2)}, u32[]{:S(2)}) collective-permute-start(bf16[512,1024]{1,0:T(8,128)(2,1)} %get-tuple-element.172), channel_id=1, source_target_pairs={{0,1},{1,0},{2,3},{3,2},{4,5},{5,4},{6,7},{7,6}} | collective-permute-start | bytes 3145736 | tf_op jit(solution)/shard_map/ppermute | solution.py:446
  219.3 90.7 %collective-permute-start.22 = (bf16[512,1024]{1,0:T(8,128)(2,1)}, bf16[512,1024]{1,0:T(8,128)(2,1)S(1)}, u32[]{:S(2)}, u32[]{:S(2)}) collective-permute-start(bf16[512,1024]{1,0:T(8,128)(2,1)} %add_convert_fusion.7), channel_id=1, source_target_pairs={{0,4},{1,5},{2,6},{3,7},{4,0},{5,1},{6,2},{7,3}} | collective-permute-start | bytes 3145736 | tf_op jit(solution)/shard_map/ppermute | solution.py:446
  222.1 47.0 %all-to-all-start = ((f32[8,8,512]{2,1,0:T(8,128)}), f32[8,8,512]{2,1,0:T(8,128)S(1)}, u32[]{:S(2)}, u32[]{:S(2)}) async-start(f32[8,8,512]{2,1,0:T(8,128)} %gather_fusion.1), calls=%async_computation | async-start | bytes 262144 | tf_op jit(solution)/shard_map/all_to_all | solution.py:511
  227.0 85.6 %collective-permute-start.23 = (bf16[512,1024]{1,0:T(8,128)(2,1)}, bf16[512,1024]{1,0:T(8,128)(2,1)}, u32[]{:S(2)}, u32[]{:S(2)}) collective-permute-start(bf16[512,1024]{1,0:T(8,128)(2,1)} %add_convert_fusion.6), channel_id=1, source_target_pairs={{0,5},{1,4},{2,7},{3,6},{4,1},{5,0},{6,3},{7,2}} | collective-permute-start | bytes 3145736 | tf_op jit(solution)/shard_map/ppermute | solution.py:446
  231.7 81.0 %collective-permute-start.24 = (bf16[512,1024]{1,0:T(8,128)(2,1)}, bf16[512,1024]{1,0:T(8,128)(2,1)}, u32[]{:S(2)}, u32[]{:S(2)}) collective-permute-start(bf16[512,1024]{1,0:T(8,128)(2,1)} %add_convert_fusion.5), channel_id=1, source_target_pairs={{0,6},{1,7},{2,4},{3,5},{4,2},{5,3},{6,0},{7,1}} | collective-permute-start | bytes 3145736 | tf_op jit(solution)/shard_map/ppermute | solution.py:446
  269.2 43.5 %collective-permute-start.25 = (bf16[512,1024]{1,0:T(8,128)(2,1)}, bf16[512,1024]{1,0:T(8,128)(2,1)}, u32[]{:S(2)}, u32[]{:S(2)}) collective-permute-start(bf16[512,1024]{1,0:T(8,128)(2,1)} %add_convert_fusion.4), channel_id=1, source_target_pairs={{0,7},{1,6},{2,5},{3,4},{4,3},{5,2},{6,1},{7,0}} | collective-permute-start | bytes 3145736 | tf_op jit(solution)/shard_map/ppermute | solution.py:446
  312.7 62.2 %collective-permute-start.26 = (bf16[512,1024]{1,0:T(8,128)(2,1)}, bf16[512,1024]{1,0:T(8,128)(2,1)}, u32[]{:S(2)}, u32[]{:S(2)}) collective-permute-start(bf16[512,1024]{1,0:T(8,128)(2,1)} %add_convert_fusion.3), channel_id=1, source_target_pairs={{0,2},{1,3},{2,0},{3,1},{4,6},{5,7},{6,4},{7,5}} | collective-permute-start | bytes 3145736 | tf_op jit(solution)/shard_map/ppermute | solution.py:446
  316.4 58.5 %collective-permute-start.27 = (bf16[512,1024]{1,0:T(8,128)(2,1)}, bf16[512,1024]{1,0:T(8,128)(2,1)}, u32[]{:S(2)}, u32[]{:S(2)}) collective-permute-start(bf16[512,1024]{1,0:T(8,128)(2,1)} %add_convert_fusion.2), channel_id=1, source_target_pairs={{0,3},{1,2},{2,1},{3,0},{4,7},{5,6},{6,5},{7,4}} | collective-permute-start | bytes 3145736 | tf_op jit(solution)/shard_map/ppermute | solution.py:446
  317.8 50.9 %all-to-all-start.1 = ((f32[8,32,512]{2,1,0:T(8,128)}), f32[8,32,512]{2,1,0:T(8,128)S(1)}, u32[]{:S(2)}, u32[]{:S(2)}) async-start(f32[8,32,512]{2,1,0:T(8,128)} %broadcast_in_dim.27), calls=%async_computation.1 | async-start | bytes 1048576 | tf_op jit(solution)/shard_map/all_to_all | solution.py:516
  (31 other events, 620.8 us)
